TPU v7x, 32 devices: a whole 2x2x4 slice. The times are simulated.
32 devices in a mesh: zero: 4 (over z), model: 4 (over x, core), trial: 2 (over y).
Axes of the slice: x: 2, y: 2, z: 4, core: 2. Of those that a mesh axis runs over, the one named last changes fastest.
Arguments:
- w_query: bfloat16 [4096, 2048], P(('trial', 'zero'), 'model'), parts along dimension 0, may hold values from -0.125 to 0.125
- low_query: bfloat16 [4096, 32], P(('trial', 'zero')), parts along dimension 0, may hold values from -0.125 to 0.125
- high_query: bfloat16 [64, 2048], P('trial', 'model'), parts along dimension 0, may hold values from -1 to 1
- w_key: bfloat16 [4096, 512], P(('trial', 'zero'), 'model'), parts along dimension 0, may hold values from -0.125 to 0.125
- low_key: bfloat16 [4096, 32], P(('trial', 'zero')), parts along dimension 0, may hold values from -0.125 to 0.125
- high_key: bfloat16 [64, 512], P('trial', 'model'), parts along dimension 0, may hold values from -1 to 1
- w_value: bfloat16 [4096, 512], P(('trial', 'zero'), 'model'), parts along dimension 0, may hold values from -0.125 to 0.125
- low_value: bfloat16 [4096, 32], P(('trial', 'zero')), parts along dimension 0, may hold values from -0.125 to 0.125
- high_value: bfloat16 [64, 512], P('trial', 'model'), parts along dimension 0, may hold values from -1 to 1
- w_mixed: bfloat16 [4096, 2048], P(('trial', 'model'), 'zero'), parts along dimension 0, may hold values from -0.125 to 0.125
- low_mixed: bfloat16 [4096, 32], P(('trial', 'model')), parts along dimension 0, may hold values from -0.125 to 0.125
- high_mixed: bfloat16 [64, 2048], P('trial', 'zero'), parts along dimension 0, may hold values from -1 to 1
- norm_train: float32 [4096], P(('trial', 'zero', 'model')), parts along dimension 0, may hold values from 0.25 to 1.75
- norm_step: float32 [4096], P(('trial', 'zero', 'model')), parts along dimension 0, may hold values from -0.3 to 0.3
Outputs:
- final_query: bfloat16 [4096, 2048], P('trial', 'model'), parts along dimension 0
- final_key: bfloat16 [4096, 512], P('trial', 'model'), parts along dimension 0
- final_value: bfloat16 [4096, 512], P('trial', 'model'), parts along dimension 0
- final_mixed: bfloat16 [4096, 2048], P(('trial', 'model')), parts along dimension 0
- serve_norm: bfloat16 [4096], P('trial'), parts along dimension 0
There are 2 independent parts, one for each index of `trial`. A program takes and returns all parts, laid end to end along the dimension named above; each array names one. Nothing has to cross between parts.
All inputs are finite; a program needn't handle non-finite values.
Results may differ from a plain program's by a relative error of at most 0.001.
Values may be sent and summed in bfloat16 or wider, within the bound.
No kernel may reach another device: no remote copies, remote signals or barrier semaphores. Data moves between devices by JAX's collectives and lax.ppermute only.
A program may use at most 64 MiB of HBM per device.

v0:
```python
import jax
import jax.numpy as jnp
from jax import lax
from jax.sharding import PartitionSpec as P

mix_rate = 2.0


def shards(
    w_query,
    low_query,
    high_query,
    w_key,
    low_key,
    high_key,
    w_value,
    low_value,
    high_value,
    w_mixed,
    low_mixed,
    high_mixed,
    norm_train,
    norm_step,
):
    result_query = w_query.astype(jnp.float32) + mix_rate * jnp.dot(
        low_query, high_query, preferred_element_type=jnp.float32
    )
    result_key = w_key.astype(jnp.float32) + mix_rate * jnp.dot(
        low_key, high_key, preferred_element_type=jnp.float32
    )
    result_value = w_value.astype(jnp.float32) + mix_rate * jnp.dot(
        low_value, high_value, preferred_element_type=jnp.float32
    )
    result_mixed = w_mixed.astype(jnp.float32) + mix_rate * jnp.dot(
        low_mixed, high_mixed, preferred_element_type=jnp.float32
    )
    narrow_query, narrow_key, narrow_value, narrow_mixed = (
        result_query.astype(jnp.bfloat16),
        result_key.astype(jnp.bfloat16),
        result_value.astype(jnp.bfloat16),
        result_mixed.astype(jnp.bfloat16),
    )
    final_query, final_key, final_value, final_mixed = (
        lax.all_gather(narrow_query, "zero", axis=0, tiled=True),
        lax.all_gather(narrow_key, "zero", axis=0, tiled=True),
        lax.all_gather(narrow_value, "zero", axis=0, tiled=True),
        lax.all_gather(narrow_mixed, "zero", axis=1, tiled=True),
    )
    serve_norm = lax.all_gather(
        (norm_train + norm_step).astype(jnp.bfloat16), ("zero", "model"), axis=0, tiled=True
    )
    return (final_query, final_key, final_value, final_mixed, serve_norm)


def solution(mesh):
    placed = (
        P(("trial", "zero"), "model"),
        P(("trial", "zero"), None),
        P("trial", "model"),
        P(("trial", "zero"), "model"),
        P(("trial", "zero"), None),
        P("trial", "model"),
        P(("trial", "zero"), "model"),
        P(("trial", "zero"), None),
        P("trial", "model"),
        P(("trial", "model"), "zero"),
        P(("trial", "model"), None),
        P("trial", "zero"),
        P(("trial", "zero", "model")),
        P(("trial", "zero", "model")),
    )
    return jax.shard_map(
        shards,
        mesh=mesh,
        in_specs=placed,
        out_specs=(
            P("trial", "model"),
            P("trial", "model"),
            P("trial", "model"),
            P(("trial", "model"), None),
            P("trial"),
        ),
        check_vma=False,
    )
```

profile of v0, /device:TPU:0, one launch (start us, length us, event | category | flops | bytes accessed | tf_op | source)
XLA Modules:
  0.0 131.7 jit_solution(212639038545267897)
XLA Ops:
  7.2 0.0 copy-start
  7.2 0.0 copy-start.2
  7.2 0.0 copy-start.4
  7.2 0.0 copy-start.6
  7.2 0.0 copy-start.3
  7.2 0.0 copy-start.5
  7.2 0.0 all-gather.4.cloned.1.call-start
  7.3 0.6 copy-done
  7.9 2.2 %fusion.2 = bf16[512,512]{1,0:T(8,128)(2,1)} fusion(bf16[512,32]{0,1:T(8,128)(2,1)S(1)} %copy-done, bf16[32,512]{1,0:T(8,128)(2,1)} %param.16, bf16[512,512]{1,0:T(8,128)(2,1)} %param.14), kind=kOutput, calls=%fused_computation.4 | convolution fusion | flops 17825792 | bytes 1114112 | tf_op jit(solution)/shard_map/dot_general | solution.py:25
  10.1 0.0 all-gather.4.cloned.1.call-update
  10.1 0.0 all-gather.6.cloned.1.call-start
  10.2 2.2 %fusion.3 = bf16[512,512]{1,0:T(8,128)(2,1)} fusion(bf16[512,32]{0,1:T(8,128)(2,1)} %param.24, bf16[32,512]{1,0:T(8,128)(2,1)} %param.25, bf16[512,512]{1,0:T(8,128)(2,1)} %param.23), kind=kOutput, calls=%fused_computation.5 | convolution fusion | flops 17825792 | bytes 1114112 | tf_op jit(solution)/shard_map/dot_general | solution.py:34
  12.4 0.0 all-gather.6.cloned.1.call-update
  12.4 0.2 fusion.6
  12.7 23.1 %all_gather.16 = bf16[2048,128]{1,0:T(8,128)(2,1)S(1)} all-gather(bf16[512,128]{1,0:T(8,128)(2,1)S(1)} %fusion.6), channel_id=1, replica_groups=mesh['zero'=4,'model'=4,'trial'=2] {'zero'}, dimensions={0}, use_global_device_ids=true | all-gather | bytes 655360 | tf_op jit(solution)/shard_map/all_gather | solution.py:45
  35.8 0.2 fusion.7
  36.0 21.4 %all_gather.17 = bf16[2048,128]{1,0:T(8,128)(2,1)S(1)} all-gather(bf16[512,128]{1,0:T(8,128)(2,1)S(1)} %fusion.7), channel_id=1, replica_groups=mesh['zero'=4,'model'=4,'trial'=2] {'zero'}, dimensions={0}, use_global_device_ids=true | all-gather | bytes 655360 | tf_op jit(solution)/shard_map/all_gather | solution.py:46
  57.4 20.5 %all-gather = bf16[16,1,128]{2,1,0:T(2,128)(2,1)S(1)} all-gather(bf16[1,1,128]{2,1,0:T(2,128)(2,1)S(1)} %convert_bitcast_fusion), channel_id=1, replica_groups=mesh['zero'=4,'model'=4,'trial'=2] {'zero','model'}, dimensions={0}, use_global_device_ids=true | all-gather | bytes 4352 | tf_op jit(solution)/shard_map/all_gather | solution.py:49
  77.9 0.6 reduce
  78.5 40.3 %all-gather.6.cloned.1.call-done = bf16[512,2048]{1,0:T(8,128)(2,1)} async-done(((bf16[512,512]{1,0:T(8,128)(2,1)}), bf16[512,2048]{1,0:T(8,128)(2,1)}) %all-gather.6.cloned.1.call-update) | async-done | bytes 2097168 | tf_op jit(solution)/shard_map/all_gather | solution.py:47
  118.8 3.2 %copy.23 = bf16[2048,512]{1,0:T(8,128)(2,1)} copy(bf16[2048,512]{1,0:T(8,128)(2,1)} %all-gather.4.cloned.1.call-done) | data formatting | bytes 4194304
  122.0 0.8 copy.24
  122.8 0.8 copy.25
  123.6 1.3 %copy.26 = bf16[512,2048]{1,0:T(8,128)(2,1)} copy(bf16[512,2048]{1,0:T(8,128)(2,1)S(1)} %copy-done.1) | data formatting | bytes 4194304
  (15 shorter events, 0.0 us)
Async XLA Ops:
  7.2 0.8 copy-start
  7.2 5.2 %copy-start.2 = (bf16[512,128]{1,0:T(8,128)(2,1)S(1)}, bf16[512,128]{1,0:T(8,128)(2,1)}, u32[]{:S(2)}) copy-start(bf16[512,128]{1,0:T(8,128)(2,1)} %param.17) | copy-start | bytes 393220
  7.2 5.2 %copy-start.4 = (bf16[512,32]{0,1:T(8,128)(2,1)S(1)}, bf16[512,32]{0,1:T(8,128)(2,1)}, u32[]{:S(2)}) copy-start(bf16[512,32]{0,1:T(8,128)(2,1)} %param.18) | copy-start | bytes 98308
  7.2 5.2 %copy-start.6 = (bf16[32,128]{1,0:T(8,128)(2,1)S(1)}, bf16[32,128]{1,0:T(8,128)(2,1)}, u32[]{:S(2)}) copy-start(bf16[32,128]{1,0:T(8,128)(2,1)} %param.19) | copy-start | bytes 24580
  7.2 28.6 %copy-start.3 = (bf16[512,128]{1,0:T(8,128)(2,1)S(1)}, bf16[512,128]{1,0:T(8,128)(2,1)}, u32[]{:S(2)}) copy-start(bf16[512,128]{1,0:T(8,128)(2,1)} %param.20) | copy-start | bytes 393220
  7.2 28.6 %copy-start.5 = (bf16[512,32]{0,1:T(8,128)(2,1)S(1)}, bf16[512,32]{0,1:T(8,128)(2,1)}, u32[]{:S(2)}) copy-start(bf16[512,32]{0,1:T(8,128)(2,1)} %param.21) | copy-start | bytes 98308
  7.2 28.5 %copy-start.7 = (bf16[32,128]{1,0:T(8,128)(2,1)S(1)}, bf16[32,128]{1,0:T(8,128)(2,1)}, u32[]{:S(2)}) copy-start(bf16[32,128]{1,0:T(8,128)(2,1)} %param.22) | copy-start | bytes 24580
  7.2 71.2 %all-gather.4.cloned.1.call-start = ((), (), s32[]{:S(2)}) async-start(), calls=%async_computation | async-start | bytes 2621440 | tf_op jit(solution)/shard_map/all_gather | solution.py:44
  10.1 47.3 %copy-start.8 = (f32[128]{0:T(128)S(1)}, f32[128]{0:T(128)}, u32[]{:S(2)}) copy-start(f32[128]{0:T(128)} %param.26) | copy-start | bytes 1540
  10.1 47.3 %copy-start.9 = (f32[128]{0:T(128)S(1)}, f32[128]{0:T(128)}, u32[]{:S(2)}) copy-start(f32[128]{0:T(128)} %param.27) | copy-start | bytes 1540
  10.1 108.7 %all-gather.6.cloned.1.call-start = ((), (), s32[]{:S(2)}) async-start(), calls=%async_computation.1 | async-start | bytes 2621440 | tf_op jit(solution)/shard_map/all_gather | solution.py:47
  118.8 4.8 %copy-start.1 = (bf16[512,2048]{1,0:T(8,128)(2,1)S(1)}, bf16[512,2048]{1,0:T(8,128)(2,1)}, u32[]{:S(2)}) copy-start(bf16[512,2048]{1,0:T(8,128)(2,1)} %all-gather.6.cloned.1.call-done) | copy-start | bytes 6291460
Sparse Core Ops, SparseCore 0:
  10.3 60.5 all-gather.3
  73.0 45.7 all-gather.5
where the time goes:
time: 132 us
  blocking collectives  65 us (49%)
  waiting for transfers between devices  40.3 us (31%)
  between operations  14.2 us (11%)
  local copies, waits for them, and re-layouts  6.78 us (5%)
  matrix products  4.8 us (4%)
    all_gather x1, waiting for transfers between devices, shards(): lax.all_gather(narrow_mixed, 'zero', axis=1, tiled=True)  40.3 us
    all_gather x1, blocking collectives, shards(): lax.all_gather(narrow_key, 'zero', axis=0, tiled=True)  23.1 us
    all_gather x1, blocking collectives, shards(): lax.all_gather(narrow_value, 'zero', axis=0, tiled=True)  21.4 us
    all_gather x1, blocking collectives, shards(): lax.all_gather((norm_train + norm_step).astype(jnp.bfloat16), ('zero', 'm...  20.5 us
    unnamed x24, local copies, waits for them, and re-layouts  6.78 us
  transfers between devices with their start and end apart: 2, of which 1 were waited for; matrix products, arithmetic and copies ran while one was open for 2% of the time, Pallas kernels for 0%

commit v1 on v0

v1 whole, which is shorter than its diff:
```python
import jax
import jax.numpy as jnp
from jax import lax
from jax.experimental import pallas as pl
from jax.experimental.pallas import tpu as pltpu
from jax.sharding import PartitionSpec as P

mix_rate = 2.0
pieces = 4


def split(size):
    return size // pieces if size % (16 * pieces) == 0 else size


def merge(parts):
    count = len(parts)
    rows = sum(p[4] for p in parts)
    width = parts[0][0].shape[1]

    def body(*refs):
        ins, out, scratch, sems = refs[: 3 * count], refs[3 * count], refs[3 * count + 1 : -1], refs[-1]

        def factor(p, j):
            return pltpu.make_async_copy(ins[3 * p + j], scratch[3 * p + j], sems.at[p, pieces + j - 1])

        def base(p, i):
            first, size = parts[p][3:]
            step = split(size)
            return pltpu.make_async_copy(
                ins[3 * p].at[pl.ds(first + i * step, step)], scratch[3 * p].at[pl.ds(i * step, step)], sems.at[p, i]
            )

        for p in range(count):
            factor(p, 1).start()
            factor(p, 2).start()
        for p in range(count):
            for i in range(parts[p][4] // split(parts[p][4])):
                base(p, i).start()
        products = []
        for p, (_, _, _, first, size) in enumerate(parts):
            factor(p, 1).wait()
            factor(p, 2).wait()
            products.append(
                lax.dot_general(
                    scratch[3 * p + 1][:, first : first + size],
                    scratch[3 * p + 2][...],
                    (((0,), (0,)), ((), ())),
                    preferred_element_type=jnp.float32,
                )
            )
        start = 0
        for p in range(count):
            size = parts[p][4]
            for i in range(size // split(size)):
                base(p, i).wait()
            merged = scratch[3 * p][...].astype(jnp.float32) + mix_rate * products[p]
            out[start : start + size, :] = merged.astype(jnp.bfloat16)
            start += size

    flat = [pltpu.with_memory_space_constraint(a, pltpu.HBM) for part in parts for a in part[:3]]
    scratch = [
        pltpu.VMEM(shape, jnp.bfloat16)
        for w, low, high, _, size in parts
        for shape in ((size, w.shape[1]), low.shape, high.shape)
    ]
    return pl.pallas_call(
        body,
        in_specs=[pl.BlockSpec(memory_space=pltpu.HBM)] * len(flat),
        out_specs=pl.BlockSpec(memory_space=pltpu.VMEM),
        out_shape=pltpu.VMEM((rows, width), jnp.bfloat16),
        scratch_shapes=scratch + [pltpu.SemaphoreType.DMA((count, pieces + 2))],
        compiler_params=pltpu.CompilerParams(vmem_limit_bytes=16 * 2**20),
    )(*flat)


def place(outs, shapes, moves):
    chunks = [pltpu.with_memory_space_constraint(m[0], pltpu.VMEM) for m in moves]
    given = [] if outs is None else list(outs)

    def body(*refs):
        got = refs[: len(chunks)]
        out = refs[len(chunks) + len(given) : -1]
        sems = refs[-1]
        position, zeros = lax.axis_index("zero"), lax.axis_size("zero")

        def each(act):
            for i, (_, kind, shard, there) in enumerate(moves):

                @pl.when(there(position))
                def _(i=i, kind=kind, shard=shard):
                    base = 0
                    for j, (o, axis, first, size) in enumerate(kind):
                        block = shapes[o].shape[axis] // zeros
                        start = pl.multiple_of(shard(position) * block, block)
                        if axis == 0:
                            target = out[o].at[pl.ds(pl.multiple_of(start + first, size), size), :]
                        else:
                            target = out[o].at[pl.ds(first, size), pl.ds(start, block)]
                        step = split(size)
                        for r in range(0, size, step):
                            act(
                                pltpu.make_async_copy(
                                    got[i].at[pl.ds(base + r, step), :],
                                    target.at[pl.ds(r, step), :],
                                    sems.at[i, j, r // step],
                                )
                            )
                        base += size

        each(lambda c: c.start())
        each(lambda c: c.wait())

    return pl.pallas_call(
        body,
        in_specs=[pl.BlockSpec(memory_space=pltpu.VMEM)] * len(chunks)
        + [pl.BlockSpec(memory_space=pl.ANY)] * len(given),
        out_specs=[pl.BlockSpec(memory_space=pl.ANY)] * len(shapes),
        out_shape=list(shapes),
        input_output_aliases={len(chunks) + o: o for o in range(len(given))},
        scratch_shapes=[pltpu.SemaphoreType.DMA((len(moves), 2, pieces))],
        compiler_params=pltpu.CompilerParams(vmem_limit_bytes=2**20),
    )(*chunks, *given)


def plan(query, key, mixed):
    return [
        [(1, 0, 0, key[0]), (2, 0, 0, key[0])],
        [(3, 1, 0, mixed[0])],
        [(0, 0, 0, query[0])],
    ]


def solution(mesh):
    zeros, models, trials = (mesh.shape[n] for n in ("zero", "model", "trial"))
    even = [(i, i ^ 1) for i in range(zeros) if (i ^ 1) < zeros]
    odd = [(i, (i + 1 ^ 1) - 1) for i in range(zeros) if 0 <= (i + 1 ^ 1) - 1 < zeros]

    def source(i, side, step):
        sign = (1 - 2 * (i % 2)) * (1 - 2 * side)
        return i + sign * step

    def live(side, step):
        return [(a, b) for a, b in (even, odd)[side] if 0 <= source(b, side, step) < zeros]

    def hops(axis, size):
        return [(axis, size, 1 << k) for k in range((size - 1).bit_length())] if size & (size - 1) == 0 else [(axis, size, 0)]

    spread = hops("model", models) + hops("zero", zeros)


    def run(*args):
        wq, wk, wm = args[0], args[3], args[9]
        chunks = plan(
            (wq.shape[0] // (trials * zeros), wq.shape[1] // models),
            (wk.shape[0] // (trials * zeros), wk.shape[1] // models),
            (wm.shape[0] // (trials * models), wm.shape[1] // zeros),
        )
        count = len(chunks)

        def shards(*own):
            position = lax.axis_index("zero")
            given = [(own[3 * o], own[3 * o + 1].T, own[3 * o + 2]) for o in range(4)]
            shapes = [
                jax.ShapeDtypeStruct((w.shape[0] * (1 if o == 3 else zeros), w.shape[1] * (zeros if o == 3 else 1)), w.dtype)
                for o, (w, _, _) in enumerate(given)
            ]
            merged = []
            for parts in chunks:
                merged.append(merge([(*given[o], first, size) for o, _, first, size in parts]))
            outs = place(None, shapes, [(merged[c], chunks[c], lambda i: i, lambda i: i >= 0) for c in range(count)])
            held = [[m, m] for m in merged]
            for step in range(1, zeros):
                arrived = []
                for c in range(count):
                    fresh = [None, None]
                    for side in (0, 1):
                        pairs = live(side, step)
                        if pairs:
                            fresh[side] = lax.ppermute(held[c][1 - side], "zero", pairs)

                            def shard(i, side=side, step=step):
                                return source(i, side, step)

                            def there(i, side=side, step=step):
                                return (source(i, side, step) >= 0) & (source(i, side, step) < zeros)

                            arrived.append((fresh[side], chunks[c], shard, there))
                    held[c] = fresh
                if step < zeros - 1:
                    outs = place(outs, shapes, arrived)
                else:
                    for one in arrived:
                        outs = place(outs, shapes, [one])

            norm_train, norm_step = own[12:]
            gain = (norm_train + norm_step).astype(jnp.bfloat16)
            slot = position * models + lax.axis_index("model")
            rows = jnp.where(lax.broadcasted_iota(jnp.int32, (zeros * models, 1), 0) == slot, gain[None, :], 0)
            for axis, size, hop in spread:
                if hop:
                    rows = rows + lax.ppermute(rows, axis, [(i, i ^ hop) for i in range(size)])
                else:
                    rows = lax.psum(rows, axis)
            return (*outs, rows.reshape(-1))

        tall = [P(("trial", "zero"), "model"), P(("trial", "zero"), None), P("trial", "model")]
        wide = [P(("trial", "model"), "zero"), P(("trial", "model"), None), P("trial", "zero")]
        gains = [P(("trial", "zero", "model"))] * 2
        step = jax.shard_map(
            shards,
            mesh=mesh,
            in_specs=tuple(tall * 3 + wide + gains),
            out_specs=(*[P("trial", "model")] * 3, P(("trial", "model"), None), P("trial")),
            check_vma=False,
        )
        return step(*args)

    return run
```

time: 132 us -> 134 us (1.015)
  blocking collectives: 65 us -> 0 us
  waiting for transfers between devices: 40.3 us -> 99.9 us
  starting transfers between devices: 0.08 us -> 21.4 us
  between operations: 14.2 us -> 0.96 us
  Pallas kernels: 0 us -> 10.8 us
  local copies, waits for them, and re-layouts: 6.78 us -> 0.01 us
  matrix products: 4.8 us -> 0 us
    ppermute x0 -> x19, waiting for transfers between devices: none -> 99.9 us  [the longest x15 76.7 us: shards(): fresh[side] = lax.ppermute(held[c][1 - side], 'zero', pairs)]
    all_gather x3 -> x0, blocking collectives: 65 us -> none  [the longest x1 23.1 us: shards(): lax.all_gather(narrow_key, 'zero', axis=0, tiled=True)]
    all_gather x2 -> x0, waiting for transfers between devices: 40.3 us -> none  [the longest x1 40.3 us: shards(): lax.all_gather(narrow_mixed, 'zero', axis=1, tiled=True)]
    ppermute x0 -> x19, starting transfers between devices: none -> 21.4 us  [the longest x15 17.1 us: shards(): fresh[side] = lax.ppermute(held[c][1 - side], 'zero', pairs)]
    pallas_call x0 -> x9, Pallas kernels: none -> 10.8 us  [the longest x6 6.73 us: place(): pl.pallas_call(body, in_specs=[pl.BlockSpec(memory_space=pltpu.VMEM)] * l...]
    unnamed x24 -> x4, local copies, waits for them, and re-layouts: 6.78 us -> 0.01 us
    dot_general x4 -> x0, matrix products: 4.8 us -> none  [the longest x1 2.2 us: shards(): jnp.dot(low_mixed, high_mixed, preferred_element_type=jnp.float32)]
  transfers between devices with their start and end apart: 2 -> 19, of which waited for: 1 -> 5; matrix products, arithmetic and copies ran while one was open for 2% -> 1% of each run, Pallas kernels for 0% -> 6%
where the time goes in v1:
time: 134 us
  waiting for transfers between devices  99.9 us (75%)
  starting transfers between devices  21.4 us (16%)
  Pallas kernels  10.8 us (8%)
    ppermute x15, waiting for transfers between devices, shards(): fresh[side] = lax.ppermute(held[c][1 - side], 'zero', pairs)  76.7 us
    ppermute x4, waiting for transfers between devices, shards(): rows = rows + lax.ppermute(rows, axis, [(i, i ^ hop) for i in range(size)])  23.2 us
    ppermute x15, starting transfers between devices, shards(): fresh[side] = lax.ppermute(held[c][1 - side], 'zero', pairs)  17.1 us
    pallas_call x6, Pallas kernels, place(): pl.pallas_call(body, in_specs=[pl.BlockSpec(memory_space=pltpu.VMEM)] * l...  6.73 us
    ppermute x4, starting transfers between devices, shards(): rows = rows + lax.ppermute(rows, axis, [(i, i ^ hop) for i in range(size)])  4.3 us
    pallas_call x3, Pallas kernels, merge(): pl.pallas_call(body, in_specs=[pl.BlockSpec(memory_space=pltpu.HBM)] * le...  4.05 us
  transfers between devices with their start and end apart: 19, of which 5 were waited for; matrix products, arithmetic and copies ran while one was open for 1% of the time, Pallas kernels for 6%

profile of v1, /device:TPU:0, one launch (start us, length us, event | category | flops | bytes accessed | tf_op | source)
XLA Modules:
  0.0 133.9 jit_solution(5570800648866827758)
XLA Ops:
  0.7 1.3 shard_map.173.refs_2_
  2.0 3.1 %collective-permute-start = (bf16[512,512]{1,0:T(8,128)(2,1)S(1)}, bf16[512,512]{1,0:T(8,128)(2,1)S(1)}, u32[]{:S(2)}, u32[]{:S(2)}) collective-permute-start(bf16[512,512]{1,0:T(8,128)(2,1)S(1)} %shard_map.173.refs_2_), channel_id=1, source_target_pairs={{0,8},{8,0},{16,24},{24,16},{1,9},{9,1},{17,25},{25,17},{2,10},{10... | collective-permute-start | bytes 1572872 | tf_op jit(solution)/shard_map/ppermute | solution.py:180
  5.1 1.3 shard_map.174.refs_1_
  6.6 1.4 %shard_map.175.refs_0_ = bf16[1024,128]{1,0:T(8,128)(2,1)S(1)} custom-call(bf16[512,128]{1,0:T(8,128)(2,1)} %refs_0_.5, bf16[32,512]{1,0:T(8,128)(2,1)} %bitcast.8, bf16[32,128]{1,0:T(8,128)(2,1)} %refs_2_.5, bf16[512,128]{1,0:T(8,128)(2,1)} %refs_3_.1, bf16[32,512]{1,0:T(8,128)(2,1)} %bitcast.9, bf16[32,128]{1,0:T(8,128)(2,1)} %refs_5_.1), custom_call_target="tpu_custom_call" | custom-call | tf_op jit(solution)/shard_map/pallas_call | solution.py:67
  8.1 2.1 %collective-permute-start.6 = (bf16[1024,128]{1,0:T(8,128)(2,1)S(1)}, bf16[1024,128]{1,0:T(8,128)(2,1)S(1)}, u32[]{:S(2)}, u32[]{:S(2)}) collective-permute-start(bf16[1024,128]{1,0:T(8,128)(2,1)S(1)} %shard_map.175.refs_0_), channel_id=1, source_target_pairs={{0,8},{8,0},{16,24},{24,16},{1,9},{9,1},{17,25},{25,17},{2,10},{10... | collective-permute-start | bytes 786440 | tf_op jit(solution)/shard_map/ppermute | solution.py:180
  10.2 1.5 %collective-permute-start.16 = (bf16[16,128]{1,0:T(8,128)(2,1)S(1)}, bf16[16,128]{1,0:T(8,128)(2,1)S(1)}, u32[]{:S(2)}, u32[]{:S(2)}) collective-permute-start(bf16[16,128]{1,0:T(8,128)(2,1)S(1)} %fusion), channel_id=1, source_target_pairs={{0,4},{2,6},{4,0},{6,2},{1,5},{3,7},{5,1},{7,3},{8,12},{10,14},{12... | collective-permute-start | bytes 12296 | tf_op jit(solution)/shard_map/ppermute | solution.py:202
  11.7 2.1 %collective-permute-done.16 = bf16[16,128]{1,0:T(8,128)(2,1)S(1)} collective-permute-done((bf16[16,128]{1,0:T(8,128)(2,1)S(1)}, bf16[16,128]{1,0:T(8,128)(2,1)S(1)}, u32[]{:S(2)}, u32[]{:S(2)}) %collective-permute-start.16) | collective-permute-done | bytes 4128 | tf_op jit(solution)/shard_map/ppermute | solution.py:202
  13.9 20.0 %collective-permute-done.17 = bf16[16,128]{1,0:T(8,128)(2,1)S(1)} collective-permute-done((bf16[16,128]{1,0:T(8,128)(2,1)S(1)}, bf16[16,128]{1,0:T(8,128)(2,1)S(1)}, u32[]{:S(2)}, u32[]{:S(2)}) %collective-permute-start.17) | collective-permute-done | bytes 4128 | tf_op jit(solution)/shard_map/ppermute | solution.py:202
  34.0 2.8 %collective-permute-start.18 = (bf16[16,128]{1,0:T(8,128)(2,1)S(1)}, bf16[16,128]{1,0:T(8,128)(2,1)S(1)}, u32[]{:S(2)}, u32[]{:S(2)}) collective-permute-start(bf16[16,128]{1,0:T(8,128)(2,1)S(1)} %add.22), channel_id=1, source_target_pairs={{0,16},{8,24},{16,0},{24,8},{1,17},{9,25},{17,1},{25,9},{2,18},{10... | collective-permute-start | bytes 12296 | tf_op jit(solution)/shard_map/ppermute | solution.py:202
  37.4 1.1 collective-permute-done.18
  42.0 1.3 collective-permute-start.12
  43.3 1.3 collective-permute-start.14
  44.6 1.3 collective-permute-start.10
  45.9 1.3 collective-permute-start.5
  47.2 1.3 collective-permute-start.2
  48.5 57.5 %collective-permute-done.10.refs_0_ = bf16[1024,128]{1,0:T(8,128)(2,1)S(1)} collective-permute-done((bf16[1024,128]{1,0:T(8,128)(2,1)S(1)}, bf16[1024,128]{1,0:T(8,128)(2,1)S(1)}, u32[]{:S(2)}, u32[]{:S(2)}) %collective-permute-start.10) | collective-permute-done | bytes 262176 | tf_op jit(solution)/shard_map/ppermute | solution.py:180
  106.1 1.3 collective-permute-start.8
  107.4 1.3 shard_map.176
  109.2 1.5 %shard_map.177 = (bf16[2048,512]{1,0:T(8,128)(2,1)}, bf16[2048,128]{1,0:T(8,128)(2,1)}, bf16[2048,128]{1,0:T(8,128)(2,1)}, bf16[512,2048]{1,0:T(8,128)(2,1)}) custom-call(bf16[1024,128]{1,0:T(8,128)(2,1)S(1)} %collective-permute-done.6.refs_0_, ...), custom_call_target="tpu_custom_call", output_to_operand_aliasing={{0}: (6, {}), {1}: (7, {}), {2}: (8, {}), {3}: (9, {})} | custom-call | tf_op jit(solution)/shard_map/pallas_call | solution.py:114
  110.7 1.5 %shard_map.178 = (bf16[2048,512]{1,0:T(8,128)(2,1)}, bf16[2048,128]{1,0:T(8,128)(2,1)}, bf16[2048,128]{1,0:T(8,128)(2,1)}, bf16[512,2048]{1,0:T(8,128)(2,1)}) custom-call(bf16[1024,128]{1,0:T(8,128)(2,1)S(1)} %collective-permute-done.10.refs_0_, ...), custom_call_target="tpu_custom_call", output_to_operand_aliasing={{0}: (6, {}), {1}: (7, {}), {2}: (8, {}), {3}: (9, {})} | custom-call | tf_op jit(solution)/shard_map/pallas_call | solution.py:114
  112.2 19.1 %collective-permute-done.8.refs_0_ = bf16[1024,128]{1,0:T(8,128)(2,1)S(1)} collective-permute-done((bf16[1024,128]{1,0:T(8,128)(2,1)S(1)}, bf16[1024,128]{1,0:T(8,128)(2,1)S(1)}, u32[]{:S(2)}, u32[]{:S(2)}) %collective-permute-start.8) | collective-permute-done | bytes 262176 | tf_op jit(solution)/shard_map/ppermute | solution.py:180
  131.3 0.8 shard_map.179
  132.1 0.9 shard_map.180
  133.0 0.9 shard_map.181
  (34 shorter events, 5.1 us)
Async XLA Ops:
  0.6 5.9 %copy-start = (f32[128]{0:T(128)S(1)}, f32[128]{0:T(128)}, u32[]{:S(2)}) copy-start(f32[128]{0:T(128)} %param.26) | copy-start | bytes 1540
  0.6 5.9 %copy-start.1 = (f32[128]{0:T(128)S(1)}, f32[128]{0:T(128)}, u32[]{:S(2)}) copy-start(f32[128]{0:T(128)} %param.27) | copy-start | bytes 1540
  2.0 38.6 %collective-permute-start = (bf16[512,512]{1,0:T(8,128)(2,1)S(1)}, bf16[512,512]{1,0:T(8,128)(2,1)S(1)}, u32[]{:S(2)}, u32[]{:S(2)}) collective-permute-start(bf16[512,512]{1,0:T(8,128)(2,1)S(1)} %shard_map.173.refs_2_), channel_id=1, source_target_pairs={{0,8},{8,0},{16,24},{24,16},{1,9},{9,1},{17,25},{25,17},{2,10},{10... | collective-permute-start | bytes 1572872 | tf_op jit(solution)/shard_map/ppermute | solution.py:180
  6.4 33.5 %collective-permute-start.3 = (bf16[512,512]{1,0:T(8,128)(2,1)S(1)}, bf16[512,512]{1,0:T(8,128)(2,1)S(1)}, u32[]{:S(2)}, u32[]{:S(2)}) collective-permute-start(bf16[512,512]{1,0:T(8,128)(2,1)S(1)} %shard_map.174.refs_1_), channel_id=1, source_target_pairs={{0,8},{8,0},{16,24},{24,16},{1,9},{9,1},{17,25},{25,17},{2,10},{10... | collective-permute-start | bytes 1572872 | tf_op jit(solution)/shard_map/ppermute | solution.py:180
  6.6 3.5 %collective-permute-start.15 = (bf16[16,128]{1,0:T(8,128)(2,1)S(1)}, bf16[16,128]{1,0:T(8,128)(2,1)S(1)}, u32[]{:S(2)}, u32[]{:S(2)}) collective-permute-start(bf16[16,128]{1,0:T(8,128)(2,1)S(1)} %broadcast_select_fusion), channel_id=1, source_target_pairs={{0,2},{2,0},{4,6},{6,4},{1,3},{3,1},{5,7},{7,5},{8,10},{10,8},{12,... | collective-permute-start | bytes 12296 | tf_op jit(solution)/shard_map/ppermute | solution.py:202
  8.1 31.1 %collective-permute-start.6 = (bf16[1024,128]{1,0:T(8,128)(2,1)S(1)}, bf16[1024,128]{1,0:T(8,128)(2,1)S(1)}, u32[]{:S(2)}, u32[]{:S(2)}) collective-permute-start(bf16[1024,128]{1,0:T(8,128)(2,1)S(1)} %shard_map.175.refs_0_), channel_id=1, source_target_pairs={{0,8},{8,0},{16,24},{24,16},{1,9},{9,1},{17,25},{25,17},{2,10},{10... | collective-permute-start | bytes 786440 | tf_op jit(solution)/shard_map/ppermute | solution.py:180
  10.2 3.6 %collective-permute-start.16 = (bf16[16,128]{1,0:T(8,128)(2,1)S(1)}, bf16[16,128]{1,0:T(8,128)(2,1)S(1)}, u32[]{:S(2)}, u32[]{:S(2)}) collective-permute-start(bf16[16,128]{1,0:T(8,128)(2,1)S(1)} %fusion), channel_id=1, source_target_pairs={{0,4},{2,6},{4,0},{6,2},{1,5},{3,7},{5,1},{7,3},{8,12},{10,14},{12... | collective-permute-start | bytes 12296 | tf_op jit(solution)/shard_map/ppermute | solution.py:202
  13.9 20.1 %collective-permute-start.17 = (bf16[16,128]{1,0:T(8,128)(2,1)S(1)}, bf16[16,128]{1,0:T(8,128)(2,1)S(1)}, u32[]{:S(2)}, u32[]{:S(2)}) collective-permute-start(bf16[16,128]{1,0:T(8,128)(2,1)S(1)} %fusion.1), channel_id=1, source_target_pairs={{0,8},{8,0},{16,24},{24,16},{1,9},{9,1},{17,25},{25,17},{2,10},{10... | collective-permute-start | bytes 12296 | tf_op jit(solution)/shard_map/ppermute | solution.py:202
  34.0 4.5 %collective-permute-start.18 = (bf16[16,128]{1,0:T(8,128)(2,1)S(1)}, bf16[16,128]{1,0:T(8,128)(2,1)S(1)}, u32[]{:S(2)}, u32[]{:S(2)}) collective-permute-start(bf16[16,128]{1,0:T(8,128)(2,1)S(1)} %add.22), channel_id=1, source_target_pairs={{0,16},{8,24},{16,0},{24,8},{1,17},{9,25},{17,1},{25,9},{2,18},{10... | collective-permute-start | bytes 12296 | tf_op jit(solution)/shard_map/ppermute | solution.py:202
  36.7 5.3 %collective-permute-start.11 = (bf16[512,512]{1,0:T(8,128)(2,1)S(1)}, bf16[512,512]{1,0:T(8,128)(2,1)S(1)}, u32[]{:S(2)}, u32[]{:S(2)}) collective-permute-start(bf16[512,512]{1,0:T(8,128)(2,1)S(1)} %shard_map.174.refs_1_), channel_id=1, source_target_pairs={{8,16},{16,8},{9,17},{17,9},{10,18},{18,10},{11,19},{19,11},{12,20... | collective-permute-start | bytes 1572872 | tf_op jit(solution)/shard_map/ppermute | solution.py:180
  38.5 4.8 %collective-permute-start.13 = (bf16[512,512]{1,0:T(8,128)(2,1)S(1)}, bf16[512,512]{1,0:T(8,128)(2,1)S(1)}, u32[]{:S(2)}, u32[]{:S(2)}) collective-permute-start(bf16[512,512]{1,0:T(8,128)(2,1)S(1)} %shard_map.173.refs_2_), channel_id=1, source_target_pairs={{8,16},{16,8},{9,17},{17,9},{10,18},{18,10},{11,19},{19,11},{12,20... | collective-permute-start | bytes 1572872 | tf_op jit(solution)/shard_map/ppermute | solution.py:180
  39.2 2.1 %collective-permute-start.9 = (bf16[1024,128]{1,0:T(8,128)(2,1)S(1)}, bf16[1024,128]{1,0:T(8,128)(2,1)S(1)}, u32[]{:S(2)}, u32[]{:S(2)}) collective-permute-start(bf16[1024,128]{1,0:T(8,128)(2,1)S(1)} %shard_map.175.refs_0_), channel_id=1, source_target_pairs={{8,16},{16,8},{9,17},{17,9},{10,18},{18,10},{11,19},{19,11},{12,20... | collective-permute-start | bytes 786440 | tf_op jit(solution)/shard_map/ppermute | solution.py:180
  39.9 6.0 %collective-permute-start.4 = (bf16[512,512]{1,0:T(8,128)(2,1)S(1)}, bf16[512,512]{1,0:T(8,128)(2,1)S(1)}, u32[]{:S(2)}, u32[]{:S(2)}) collective-permute-start(bf16[512,512]{1,0:T(8,128)(2,1)S(1)} %collective-permute-done.3.refs_2_), channel_id=1, source_target_pairs={{8,16},{16,8},{9,17},{17,9},{10,18},{18,10},{11,19},{19,11},{12,20... | collective-permute-start | bytes 1572872 | tf_op jit(solution)/shard_map/ppermute | solution.py:180
  40.6 6.6 %collective-permute-start.1 = (bf16[512,512]{1,0:T(8,128)(2,1)S(1)}, bf16[512,512]{1,0:T(8,128)(2,1)S(1)}, u32[]{:S(2)}, u32[]{:S(2)}) collective-permute-start(bf16[512,512]{1,0:T(8,128)(2,1)S(1)} %collective-permute-done.refs_4_), channel_id=1, source_target_pairs={{8,16},{16,8},{9,17},{17,9},{10,18},{18,10},{11,19},{19,11},{12,20... | collective-permute-start | bytes 1572872 | tf_op jit(solution)/shard_map/ppermute | solution.py:180
  41.3 3.3 %collective-permute-start.7 = (bf16[1024,128]{1,0:T(8,128)(2,1)S(1)}, bf16[1024,128]{1,0:T(8,128)(2,1)S(1)}, u32[]{:S(2)}, u32[]{:S(2)}) collective-permute-start(bf16[1024,128]{1,0:T(8,128)(2,1)S(1)} %collective-permute-done.6.refs_0_), channel_id=1, source_target_pairs={{8,16},{16,8},{9,17},{17,9},{10,18},{18,10},{11,19},{19,11},{12,20... | collective-permute-start | bytes 786440 | tf_op jit(solution)/shard_map/ppermute | solution.py:180
  42.0 68.7 %collective-permute-start.12 = (bf16[512,512]{1,0:T(8,128)(2,1)S(1)}, bf16[512,512]{1,0:T(8,128)(2,1)S(1)}, u32[]{:S(2)}, u32[]{:S(2)}) collective-permute-start(bf16[512,512]{1,0:T(8,128)(2,1)S(1)} %collective-permute-done.11.refs_3_), channel_id=1, source_target_pairs={{8,0},{16,24},{9,1},{17,25},{10,2},{18,26},{11,3},{19,27},{12,4},{... | collective-permute-start | bytes 1572872 | tf_op jit(solution)/shard_map/ppermute | solution.py:180
  43.3 67.4 %collective-permute-start.14 = (bf16[512,512]{1,0:T(8,128)(2,1)S(1)}, bf16[512,512]{1,0:T(8,128)(2,1)S(1)}, u32[]{:S(2)}, u32[]{:S(2)}) collective-permute-start(bf16[512,512]{1,0:T(8,128)(2,1)S(1)} %collective-permute-done.13.refs_5_), channel_id=1, source_target_pairs={{8,0},{16,24},{9,1},{17,25},{10,2},{18,26},{11,3},{19,27},{12,4},{... | collective-permute-start | bytes 1572872 | tf_op jit(solution)/shard_map/ppermute | solution.py:180
  44.6 61.5 %collective-permute-start.10 = (bf16[1024,128]{1,0:T(8,128)(2,1)S(1)}, bf16[1024,128]{1,0:T(8,128)(2,1)S(1)}, u32[]{:S(2)}, u32[]{:S(2)}) collective-permute-start(bf16[1024,128]{1,0:T(8,128)(2,1)S(1)} %collective-permute-done.9.refs_1_), channel_id=1, source_target_pairs={{8,0},{16,24},{9,1},{17,25},{10,2},{18,26},{11,3},{19,27},{12,4},{... | collective-permute-start | bytes 786440 | tf_op jit(solution)/shard_map/ppermute | solution.py:180
  45.9 86.2 %collective-permute-start.5 = (bf16[512,512]{1,0:T(8,128)(2,1)S(1)}, bf16[512,512]{1,0:T(8,128)(2,1)S(1)}, u32[]{:S(2)}, u32[]{:S(2)}) collective-permute-start(bf16[512,512]{1,0:T(8,128)(2,1)S(1)} %collective-permute-done.4.refs_3_), channel_id=1, source_target_pairs={{8,0},{16,24},{9,1},{17,25},{10,2},{18,26},{11,3},{19,27},{12,4},{... | collective-permute-start | bytes 1572872 | tf_op jit(solution)/shard_map/ppermute | solution.py:180
  47.2 85.7 %collective-permute-start.2 = (bf16[512,512]{1,0:T(8,128)(2,1)S(1)}, bf16[512,512]{1,0:T(8,128)(2,1)S(1)}, u32[]{:S(2)}, u32[]{:S(2)}) collective-permute-start(bf16[512,512]{1,0:T(8,128)(2,1)S(1)} %collective-permute-done.1.refs_5_), channel_id=1, source_target_pairs={{8,0},{16,24},{9,1},{17,25},{10,2},{18,26},{11,3},{19,27},{12,4},{... | collective-permute-start | bytes 1572872 | tf_op jit(solution)/shard_map/ppermute | solution.py:180
  106.1 25.2 %collective-permute-start.8 = (bf16[1024,128]{1,0:T(8,128)(2,1)S(1)}, bf16[1024,128]{1,0:T(8,128)(2,1)S(1)}, u32[]{:S(2)}, u32[]{:S(2)}) collective-permute-start(bf16[1024,128]{1,0:T(8,128)(2,1)S(1)} %collective-permute-done.7.refs_1_), channel_id=1, source_target_pairs={{8,0},{16,24},{9,1},{17,25},{10,2},{18,26},{11,3},{19,27},{12,4},{... | collective-permute-start | bytes 786440 | tf_op jit(solution)/shard_map/ppermute | solution.py:180

commit v2 on v0

v2 whole, which is shorter than its diff:
```python
import jax
import jax.numpy as jnp
from jax import lax
from jax.experimental import pallas as pl
from jax.experimental.pallas import tpu as pltpu
from jax.sharding import PartitionSpec as P

mix_rate = 2.0
lanes = 128


def merge(parts):
    count = len(parts)
    rows, width = parts[0][0].shape

    def body(*refs):
        ins, out, scratch, sems = refs[: 3 * count], refs[3 * count], refs[3 * count + 1 : -1], refs[-1]

        def copies(p):
            return [pltpu.make_async_copy(ins[3 * p + j], scratch[3 * p + j], sems.at[p, j]) for j in range(3)]

        every = [copies(p) for p in range(count)]
        for p in range(count):
            for j in (1, 2, 0):
                every[p][j].start()
        for p in range(count):
            every[p][1].wait()
            every[p][2].wait()
            product = lax.dot_general(
                scratch[3 * p + 1][...],
                scratch[3 * p + 2][...],
                (((0,), (0,)), ((), ())),
                preferred_element_type=jnp.float32,
            )
            every[p][0].wait()
            merged = scratch[3 * p][...].astype(jnp.float32) + mix_rate * product
            out[p * rows : (p + 1) * rows, :] = merged.astype(jnp.bfloat16)

    flat = [pltpu.with_memory_space_constraint(a, pltpu.HBM) for part in parts for a in part]
    return pl.pallas_call(
        body,
        in_specs=[pl.BlockSpec(memory_space=pltpu.HBM)] * len(flat),
        out_specs=pl.BlockSpec(memory_space=pltpu.VMEM),
        out_shape=pltpu.VMEM((rows * count, width), jnp.bfloat16),
        scratch_shapes=[pltpu.VMEM(a.shape, jnp.bfloat16) for a in flat] + [pltpu.SemaphoreType.DMA((count, 3))],
        compiler_params=pltpu.CompilerParams(vmem_limit_bytes=16 * 2**20),
    )(*flat)


def place(outs, shapes, moves):
    chunks = [pltpu.with_memory_space_constraint(m[0], pltpu.VMEM) for m in moves]
    given = [] if outs is None else list(outs)

    def body(*refs):
        got = refs[: len(chunks)]
        out = refs[len(chunks) + len(given) : -1]
        sems = refs[-1]
        position = lax.axis_index("zero")

        def each(act):
            for i, (_, kind, shard, there) in enumerate(moves):

                @pl.when(there(position))
                def _(i=i, kind=kind, shard=shard):
                    rows = got[i].shape[0] // len(kind)
                    target = pl.ds(pl.multiple_of(shard(position) * rows, rows), rows)
                    for j, o in enumerate(kind):
                        source = got[i].at[pl.ds(j * rows, rows), :]
                        act(pltpu.make_async_copy(source, out[o].at[target, :], sems.at[i, j]))

        each(lambda c: c.start())
        each(lambda c: c.wait())

    return pl.pallas_call(
        body,
        in_specs=[pl.BlockSpec(memory_space=pltpu.VMEM)] * len(chunks)
        + [pl.BlockSpec(memory_space=pl.ANY)] * len(given),
        out_specs=[pl.BlockSpec(memory_space=pl.ANY)] * len(shapes),
        out_shape=list(shapes),
        input_output_aliases={len(chunks) + o: o for o in range(len(given))},
        scratch_shapes=[pltpu.SemaphoreType.DMA((len(moves), 2))],
        compiler_params=pltpu.CompilerParams(vmem_limit_bytes=2**20),
    )(*chunks, *given)


def pack(high, gain, models):
    share, width = high.shape[0] // models, high.shape[1]
    blocks = width // lanes

    def body(high_ref, train, step, out, rows, gains, sems):
        first = pl.multiple_of(lax.axis_index("model") * share, share)
        copies = [
            pltpu.make_async_copy(high_ref.at[pl.ds(first, share)], rows, sems.at[0]),
            pltpu.make_async_copy(train, gains.at[0], sems.at[1]),
            pltpu.make_async_copy(step, gains.at[1], sems.at[2]),
        ]
        for c in copies:
            c.start()
        for c in copies:
            c.wait()
        out[share * blocks :, :] = jnp.broadcast_to((gains[0] + gains[1]).astype(jnp.bfloat16), (8, lanes))
        for j in range(blocks):
            out[j * share : (j + 1) * share, :] = rows[:, j * lanes : (j + 1) * lanes]

    gain = [jnp.pad(g, (0, lanes - g.shape[0]))[None, :] for g in gain]
    return pl.pallas_call(
        body,
        in_specs=[pl.BlockSpec(memory_space=pltpu.HBM)] * 3,
        out_specs=pl.BlockSpec(memory_space=pltpu.VMEM),
        out_shape=pltpu.VMEM((share * blocks + 8, lanes), jnp.bfloat16),
        scratch_shapes=[
            pltpu.VMEM((share, width), jnp.bfloat16),
            pltpu.VMEM((2, 1, lanes), jnp.float32),
            pltpu.SemaphoreType.DMA((3,)),
        ],
        compiler_params=pltpu.CompilerParams(vmem_limit_bytes=2**20),
    )(*[pltpu.with_memory_space_constraint(a, pltpu.HBM) for a in (high, *gain)])


def finish(out, shape, low, shared, moves, own, models):
    rows, width = moves[0][0].shape
    zeros = shape.shape[1] // width
    rank = low.shape[0]
    share, blocks = rank // models, width // lanes
    span = share * blocks + 8
    chunks = [pltpu.with_memory_space_constraint(m[0], pltpu.VMEM) for m in moves]
    extra = [] if own is None else [pltpu.with_memory_space_constraint(own, pltpu.HBM)]
    given = [] if out is None else [out]

    def body(*refs):
        got = list(refs[: len(chunks)])
        low_ref, shared_ref = refs[len(chunks) : len(chunks) + 2]
        target = refs[len(chunks) + 2 + len(extra) + len(given)]
        low_rows, high, done, mine, sems, more = refs[len(chunks) + 2 + len(extra) + len(given) + 1 :]
        position = lax.axis_index("zero")
        todo = [(got[i], shard, there) for i, (_, shard, there) in enumerate(moves)]
        copies = [pltpu.make_async_copy(low_ref, low_rows, more.at[0])]
        if extra:
            copies.append(pltpu.make_async_copy(refs[len(chunks) + 2], mine, more.at[1]))
            todo.append((mine, lambda i: i, lambda i: i >= 0))
        for c in copies:
            c.start()
        for m in range(models):
            for z in range(zeros):
                for j in range(blocks):
                    start = (m * zeros + z) * span + j * share
                    high[m * share : (m + 1) * share, z * width + j * lanes : z * width + (j + 1) * lanes] = shared_ref[
                        start : start + share, :
                    ]
        for c in copies:
            c.wait()

        def column(shard):
            return pl.ds(pl.multiple_of(shard(position) * width, width), width)

        def copy(i, shard):
            return pltpu.make_async_copy(done.at[i], target.at[:, column(shard)], sems.at[i])

        for i, (chunk, shard, there) in enumerate(todo):

            @pl.when(there(position))
            def _(i=i, chunk=chunk, shard=shard):
                product = lax.dot_general(
                    low_rows[...], high[:, column(shard)], (((0,), (0,)), ((), ())), preferred_element_type=jnp.float32
                )
                done[i] = (chunk[...].astype(jnp.float32) + mix_rate * product).astype(jnp.bfloat16)
                copy(i, shard).start()

        for i, (_, shard, there) in enumerate(todo):

            @pl.when(there(position))
            def _(i=i, shard=shard):
                copy(i, shard).wait()

    count = len(moves) + len(extra)
    return pl.pallas_call(
        body,
        in_specs=[pl.BlockSpec(memory_space=pltpu.VMEM)] * len(chunks)
        + [pl.BlockSpec(memory_space=pltpu.HBM), pl.BlockSpec(memory_space=pltpu.VMEM)]
        + [pl.BlockSpec(memory_space=pltpu.HBM)] * len(extra)
        + [pl.BlockSpec(memory_space=pl.ANY)] * len(given),
        out_specs=pl.BlockSpec(memory_space=pl.ANY),
        out_shape=shape,
        input_output_aliases={len(chunks) + 2 + len(extra): 0} if given else {},
        scratch_shapes=[
            pltpu.VMEM(low.shape, jnp.bfloat16),
            pltpu.VMEM((rank, shape.shape[1]), jnp.bfloat16),
            pltpu.VMEM((count, rows, width), jnp.bfloat16),
            pltpu.VMEM((rows, width) if extra else (16, lanes), jnp.bfloat16),
            pltpu.SemaphoreType.DMA((count,)),
            pltpu.SemaphoreType.DMA((2,)),
        ],
        compiler_params=pltpu.CompilerParams(vmem_limit_bytes=8 * 2**20),
    )(
        *chunks,
        pltpu.with_memory_space_constraint(low, pltpu.HBM),
        pltpu.with_memory_space_constraint(shared, pltpu.VMEM),
        *extra,
        *given,
    )


def solution(mesh):
    zeros, models = mesh.shape["zero"], mesh.shape["model"]
    even = [(i, i ^ 1) for i in range(zeros) if (i ^ 1) < zeros]
    odd = [(i, (i + 1 ^ 1) - 1) for i in range(zeros) if 0 <= (i + 1 ^ 1) - 1 < zeros]

    def source(i, side, step):
        sign = (1 - 2 * (i % 2)) * (1 - 2 * side)
        return i + sign * step

    def live(side, step):
        return [(a, b) for a, b in (even, odd)[side] if 0 <= source(b, side, step) < zeros]

    def hops(axis, size):
        return [(axis, size, 1 << k) for k in range((size - 1).bit_length())]

    spread = hops("zero", zeros) + hops("model", models)


    def shards(wq, lq, hq, wk, lk, hk, wv, lv, hv, wm, lm, hm, norm_train, norm_step):
        shapes = [jax.ShapeDtypeStruct((w.shape[0] * zeros, w.shape[1]), w.dtype) for w in (wq, wk, wv)]
        wide = jax.ShapeDtypeStruct((wm.shape[0], wm.shape[1] * zeros), wm.dtype)
        kinds = (None, (1, 2), (0,))
        shared = pack(hm, (norm_train, norm_step), models)
        narrow = merge([(wk, lk.T, hk), (wv, lv.T, hv)])
        query = merge([(wq, lq.T, hq)])
        held = [[x, x] for x in (wm, narrow, query)]
        outs = place(
            None, shapes, [(held[c][0], kinds[c], lambda i: i, lambda i: i >= 0) for c in (1, 2)]
        )
        for axis, size, hop in spread:
            other = lax.ppermute(shared, axis, [(i, i ^ hop) for i in range(size)])
            upper = (lax.axis_index(axis) & hop) != 0
            shared = jnp.concatenate([jnp.where(upper, other, shared), jnp.where(upper, shared, other)])
        span = shared.shape[0] // (zeros * models)
        gains = shared.reshape(models, zeros, span, lanes)[:, :, -1, : norm_train.shape[0]]
        mixed = None
        for step in range(1, zeros):
            arrived, raw = [], []
            for c in range(3):
                fresh = [None, None]
                for side in (0, 1):
                    pairs = live(side, step)
                    if pairs:
                        fresh[side] = lax.ppermute(held[c][1 - side], "zero", pairs)

                        def shard(i, side=side, step=step):
                            return source(i, side, step)

                        def there(i, side=side, step=step):
                            return (source(i, side, step) >= 0) & (source(i, side, step) < zeros)

                        if c == 0:
                            raw.append((fresh[side], shard, there))
                        else:
                            arrived.append((fresh[side], kinds[c], shard, there))
                held[c] = fresh
            mixed = finish(mixed, wide, lm.T, shared, raw, wm if step == 1 else None, models)
            if step < zeros - 1:
                outs = place(outs, shapes, arrived)
            else:
                for one in arrived:
                    outs = place(outs, shapes, [one])
        return (*outs, mixed, gains.transpose(1, 0, 2).reshape(-1))

    tall = [P(("trial", "zero"), "model"), P(("trial", "zero"), None), P("trial", "model")]
    wide = [P(("trial", "model"), "zero"), P(("trial", "model"), None), P("trial", "zero")]
    gains = [P(("trial", "zero", "model"))] * 2
    return jax.shard_map(
        shards,
        mesh=mesh,
        in_specs=tuple(tall * 3 + wide + gains),
        out_specs=(*[P("trial", "model")] * 3, P(("trial", "model"), None), P("trial")),
        check_vma=False,
    )
```

time: 132 us -> 123 us (0.932)
  blocking collectives: 65 us -> 0 us
  waiting for transfers between devices: 40.3 us -> 73 us
  starting transfers between devices: 0.08 us -> 26.7 us
  Pallas kernels: 0 us -> 18.4 us
  between operations: 14.2 us -> 0.95 us
  matrix products: 4.8 us -> 0 us
  local copies, waits for them, and re-layouts: 6.78 us -> 2.45 us
    ppermute x0 -> x19, waiting for transfers between devices: none -> 73 us  [the longest x15 68.3 us: shards(): fresh[side] = lax.ppermute(held[c][1 - side], 'zero', pairs)]
    all_gather x3 -> x0, blocking collectives: 65 us -> none  [the longest x1 23.1 us: shards(): lax.all_gather(narrow_key, 'zero', axis=0, tiled=True)]
    all_gather x2 -> x0, waiting for transfers between devices: 40.3 us -> none  [the longest x1 40.3 us: shards(): lax.all_gather(narrow_mixed, 'zero', axis=1, tiled=True)]
    ppermute x0 -> x19, starting transfers between devices: none -> 26.7 us  [the longest x15 18.8 us: shards(): fresh[side] = lax.ppermute(held[c][1 - side], 'zero', pairs)]
    pallas_call x0 -> x11, Pallas kernels: none -> 18.4 us  [the longest x3 8.58 us: finish(): pl.pallas_call(body, in_specs=[pl.BlockSpec(memory_space=pltpu.VMEM)] * l...]
    unnamed x24 -> x8, local copies, waits for them, and re-layouts: 6.78 us -> 1.84 us
    dot_general x4 -> x0, matrix products: 4.8 us -> none  [the longest x1 2.2 us: shards(): jnp.dot(low_mixed, high_mixed, preferred_element_type=jnp.float32)]
  transfers between devices with their start and end apart: 2 -> 19, of which waited for: 1 -> 8; matrix products, arithmetic and copies ran while one was open for 2% -> 1% of each run, Pallas kernels for 0% -> 14%
where the time goes in v2:
time: 123 us; the launch traced here: 122 us
  waiting for transfers between devices  73 us (59%)
  starting transfers between devices  26.7 us (22%)
  Pallas kernels  18.4 us (15%)
  local copies, waits for them, and re-layouts  2.45 us (2%)
    ppermute x15, waiting for transfers between devices, shards(): fresh[side] = lax.ppermute(held[c][1 - side], 'zero', pairs)  68.3 us
    ppermute x15, starting transfers between devices, shards(): fresh[side] = lax.ppermute(held[c][1 - side], 'zero', pairs)  18.8 us
    pallas_call x3, Pallas kernels, finish(): pl.pallas_call(body, in_specs=[pl.BlockSpec(memory_space=pltpu.VMEM)] * l...  8.58 us
    ppermute x4, starting transfers between devices, shards(): other = lax.ppermute(shared, axis, [(i, i ^ hop) for i in range(size)])  7.84 us
    pallas_call x5, Pallas kernels, place(): pl.pallas_call(body, in_specs=[pl.BlockSpec(memory_space=pltpu.VMEM)] * l...  6.45 us
    ppermute x4, waiting for transfers between devices, shards(): other = lax.ppermute(shared, axis, [(i, i ^ hop) for i in range(size)])  4.71 us
    pallas_call x2, Pallas kernels, merge(): pl.pallas_call(body, in_specs=[pl.BlockSpec(memory_space=pltpu.HBM)] * le...  2.6 us
  transfers between devices with their start and end apart: 19, of which 8 were waited for; matrix products, arithmetic and copies ran while one was open for 1% of the time, Pallas kernels for 14%

profile of v2, /device:TPU:0, one launch (start us, length us, event | category | flops | bytes accessed | tf_op | source)
XLA Modules:
  0.0 122.4 jit_solution(8739396055811643058)
XLA Ops:
  1.4 3.1 %collective-permute-start.13 = (bf16[40,128]{1,0:T(8,128)(2,1)S(1)}, bf16[40,128]{1,0:T(8,128)(2,1)S(1)}, u32[]{:S(2)}, u32[]{:S(2)}) collective-permute-start(bf16[40,128]{1,0:T(8,128)(2,1)S(1)} %shard_map.180), channel_id=1, source_target_pairs={{0,8},{8,0},{16,24},{24,16},{1,9},{9,1},{17,25},{25,17},{2,10},{10... | collective-permute-start | bytes 30728 | tf_op jit(solution)/shard_map/ppermute | solution.py:233
  4.5 1.7 %collective-permute-done.13 = bf16[40,128]{1,0:T(8,128)(2,1)S(1)} collective-permute-done((bf16[40,128]{1,0:T(8,128)(2,1)S(1)}, bf16[40,128]{1,0:T(8,128)(2,1)S(1)}, u32[]{:S(2)}, u32[]{:S(2)}) %collective-permute-start.13) | collective-permute-done | bytes 10272 | tf_op jit(solution)/shard_map/ppermute | solution.py:233
  6.2 3.1 %collective-permute-start.14 = (bf16[80,128]{1,0:T(8,128)(2,1)S(1)}, bf16[80,128]{1,0:T(8,128)(2,1)S(1)}, u32[]{:S(2)}, u32[]{:S(2)}) collective-permute-start(bf16[80,128]{1,0:T(8,128)(2,1)S(1)} %pad_maximum_fusion.3), channel_id=1, source_target_pairs={{0,16},{8,24},{16,0},{24,8},{1,17},{9,25},{17,1},{25,9},{2,18},{10... | collective-permute-start | bytes 61448 | tf_op jit(solution)/shard_map/ppermute | solution.py:233
  9.3 1.6 %collective-permute-start.10 = (bf16[512,512]{1,0:T(8,128)(2,1)}, bf16[512,512]{1,0:T(8,128)(2,1)S(1)}, u32[]{:S(2)}, u32[]{:S(2)}) collective-permute-start(bf16[512,512]{1,0:T(8,128)(2,1)} %refs_4_.1), channel_id=1, source_target_pairs={{0,8},{8,0},{16,24},{24,16},{1,9},{9,1},{17,25},{25,17},{2,10},{10... | collective-permute-start | bytes 1572872 | tf_op jit(solution)/shard_map/ppermute | solution.py:246
  12.7 1.5 %collective-permute-start.17 = (bf16[512,512]{1,0:T(8,128)(2,1)}, bf16[512,512]{1,0:T(8,128)(2,1)}, u32[]{:S(2)}, u32[]{:S(2)}) collective-permute-start(bf16[512,512]{1,0:T(8,128)(2,1)} %refs_4_.1), channel_id=1, source_target_pairs={{8,16},{16,8},{9,17},{17,9},{10,18},{18,10},{11,19},{19,11},{12,20... | collective-permute-start | bytes 1572872 | tf_op jit(solution)/shard_map/ppermute | solution.py:246
  14.2 1.4 %shard_map.174.refs_0_ = bf16[1024,128]{1,0:T(8,128)(2,1)S(1)} custom-call(bf16[512,128]{1,0:T(8,128)(2,1)} %refs_0_.3, bf16[32,512]{1,0:T(8,128)(2,1)} %bitcast.18, bf16[32,128]{1,0:T(8,128)(2,1)} %refs_2_.3, bf16[512,128]{1,0:T(8,128)(2,1)} %refs_3_.1, bf16[32,512]{1,0:T(8,128)(2,1)} %bitcast.19, bf16[32,128]{1,0:T(8,128)(2,1)} %refs_5_.1), custom_call_target="tpu_custom_call" | custom-call | tf_op jit(solution)/shard_map/pallas_call | solution.py:40
  15.6 2.6 %collective-permute-start.3 = (bf16[1024,128]{1,0:T(8,128)(2,1)S(1)}, bf16[1024,128]{1,0:T(8,128)(2,1)}, u32[]{:S(2)}, u32[]{:S(2)}) collective-permute-start(bf16[1024,128]{1,0:T(8,128)(2,1)S(1)} %shard_map.174.refs_0_), channel_id=1, source_target_pairs={{0,8},{8,0},{16,24},{24,16},{1,9},{9,1},{17,25},{25,17},{2,10},{10... | collective-permute-start | bytes 786440 | tf_op jit(solution)/shard_map/ppermute | solution.py:246
  18.2 1.6 %collective-permute-start.16 = (bf16[320,128]{1,0:T(8,128)(2,1)S(1)}, bf16[320,128]{1,0:T(8,128)(2,1)}, u32[]{:S(2)}, u32[]{:S(2)}) collective-permute-start(bf16[320,128]{1,0:T(8,128)(2,1)S(1)} %pad_maximum_fusion.1), channel_id=1, source_target_pairs={{0,4},{2,6},{4,0},{6,2},{1,5},{3,7},{5,1},{7,3},{8,12},{10,14},{12... | collective-permute-start | bytes 245768 | tf_op jit(solution)/shard_map/ppermute | solution.py:233
  19.8 3.1 %collective-permute-done.16 = bf16[320,128]{1,0:T(8,128)(2,1)} collective-permute-done((bf16[320,128]{1,0:T(8,128)(2,1)S(1)}, bf16[320,128]{1,0:T(8,128)(2,1)}, u32[]{:S(2)}, u32[]{:S(2)}) %collective-permute-start.16) | collective-permute-done | bytes 81952 | tf_op jit(solution)/shard_map/ppermute | solution.py:233
  24.3 1.5 %collective-permute-start.11 = (bf16[512,512]{1,0:T(8,128)(2,1)S(1)}, bf16[512,512]{1,0:T(8,128)(2,1)}, u32[]{:S(2)}, u32[]{:S(2)}) collective-permute-start(bf16[512,512]{1,0:T(8,128)(2,1)S(1)} %collective-permute-done.10.refs_0_), channel_id=1, source_target_pairs={{8,16},{16,8},{9,17},{17,9},{10,18},{18,10},{11,19},{19,11},{12,20... | collective-permute-start | bytes 1572872 | tf_op jit(solution)/shard_map/ppermute | solution.py:246
  26.5 9.0 %collective-permute-done.refs_2_ = bf16[512,512]{1,0:T(8,128)(2,1)S(1)} collective-permute-done((bf16[512,512]{1,0:T(8,128)(2,1)S(1)}, bf16[512,512]{1,0:T(8,128)(2,1)S(1)}, u32[]{:S(2)}, u32[]{:S(2)}) %collective-permute-start) | collective-permute-done | bytes 524320 | tf_op jit(solution)/shard_map/ppermute | solution.py:246
  36.2 2.7 %collective-permute-done.3.refs_0_ = bf16[1024,128]{1,0:T(8,128)(2,1)} collective-permute-done((bf16[1024,128]{1,0:T(8,128)(2,1)S(1)}, bf16[1024,128]{1,0:T(8,128)(2,1)}, u32[]{:S(2)}, u32[]{:S(2)}) %collective-permute-start.3) | collective-permute-done | bytes 262176 | tf_op jit(solution)/shard_map/ppermute | solution.py:246
  39.6 1.3 %collective-permute-start.18 = (bf16[512,512]{1,0:T(8,128)(2,1)}, bf16[512,512]{1,0:T(8,128)(2,1)}, u32[]{:S(2)}, u32[]{:S(2)}) collective-permute-start(bf16[512,512]{1,0:T(8,128)(2,1)} %collective-permute-done.17.refs_1_), channel_id=1, source_target_pairs={{8,0},{16,24},{9,1},{17,25},{10,2},{18,26},{11,3},{19,27},{12,4},{... | collective-permute-start | bytes 1572872 | tf_op jit(solution)/shard_map/ppermute | solution.py:246
  40.9 1.4 %collective-permute-start.4 = (bf16[1024,128]{1,0:T(8,128)(2,1)}, bf16[1024,128]{1,0:T(8,128)(2,1)}, u32[]{:S(2)}, u32[]{:S(2)}) collective-permute-start(bf16[1024,128]{1,0:T(8,128)(2,1)} %collective-permute-done.3.refs_0_), channel_id=1, source_target_pairs={{8,16},{16,8},{9,17},{17,9},{10,18},{18,10},{11,19},{19,11},{12,20... | collective-permute-start | bytes 786440 | tf_op jit(solution)/shard_map/ppermute | solution.py:246
  43.6 1.3 %collective-permute-start.12 = (bf16[512,512]{1,0:T(8,128)(2,1)}, bf16[512,512]{1,0:T(8,128)(2,1)S(1)}, u32[]{:S(2)}, u32[]{:S(2)}) collective-permute-start(bf16[512,512]{1,0:T(8,128)(2,1)} %collective-permute-done.11.refs_1_), channel_id=1, source_target_pairs={{8,0},{16,24},{9,1},{17,25},{10,2},{18,26},{11,3},{19,27},{12,4},{... | collective-permute-start | bytes 1572872 | tf_op jit(solution)/shard_map/ppermute | solution.py:246
  44.9 1.3 %collective-permute-start.2 = (bf16[512,512]{1,0:T(8,128)(2,1)S(1)}, bf16[512,512]{1,0:T(8,128)(2,1)S(1)}, u32[]{:S(2)}, u32[]{:S(2)}) collective-permute-start(bf16[512,512]{1,0:T(8,128)(2,1)S(1)} %collective-permute-done.1.refs_3_), channel_id=1, source_target_pairs={{8,0},{16,24},{9,1},{17,25},{10,2},{18,26},{11,3},{19,27},{12,4},{... | collective-permute-start | bytes 1572872 | tf_op jit(solution)/shard_map/ppermute | solution.py:246
  48.5 5.4 %collective-permute-done.18.refs_0_ = bf16[512,512]{1,0:T(8,128)(2,1)} collective-permute-done((bf16[512,512]{1,0:T(8,128)(2,1)}, bf16[512,512]{1,0:T(8,128)(2,1)}, u32[]{:S(2)}, u32[]{:S(2)}) %collective-permute-start.18) | collective-permute-done | bytes 524320 | tf_op jit(solution)/shard_map/ppermute | solution.py:246
  57.8 3.6 %shard_map.181.refs_4_ = bf16[512,2048]{1,0:T(8,128)(2,1)} custom-call(bf16[512,512]{1,0:T(8,128)(2,1)S(1)} %copy-done.1, bf16[512,512]{1,0:T(8,128)(2,1)} %collective-permute-done.17.refs_1_, bf16[32,512]{1,0:T(8,128)(2,1)} %bitcast.14, bf16[640,128]{1,0:T(8,128)(2,1)S(1)} %pad_maximum_fusion.refs_3_.refs_2_, bf16[512,512]{1,0:T(8,128)(2,1)} %refs_4_.1), custom_call_target="tpu_custom_call" | custom-call | tf_op jit(solution)/shard_map/pallas_call | solution.py:176
  61.4 1.9 %shard_map.176 = (bf16[2048,512]{1,0:T(8,128)(2,1)}, bf16[2048,128]{1,0:T(8,128)(2,1)}, bf16[2048,128]{1,0:T(8,128)(2,1)}) custom-call(bf16[1024,128]{1,0:T(8,128)(2,1)} %collective-permute-done.3.refs_0_, bf16[1024,128]{1,0:T(8,128)(2,1)S(1)} %copy-done.3, ...), custom_call_target="tpu_custom_call", output_to_operand_aliasing={{0}: (4, {}), {1}: (5, {}), {2}: (6, {})} | custom-call | tf_op jit(solution)/shard_map/pallas_call | solution.py:74
  63.3 3.1 %shard_map.182.refs_3_ = bf16[512,2048]{1,0:T(8,128)(2,1)} custom-call(bf16[512,512]{1,0:T(8,128)(2,1)} %collective-permute-done.18.refs_0_, bf16[512,512]{1,0:T(8,128)(2,1)} %collective-permute-done.11.refs_1_, bf16[32,512]{1,0:T(8,128)(2,1)} %bitcast.15, bf16[640,128]{1,0:T(8,128)(2,1)S(1)} %pad_maximum_fusion.refs_3_.refs_2_, ...), custom_call_target="tpu_custom_call", output_to_operand_aliasing={{}: (4, {})} | custom-call | tf_op jit(solution)/shard_map/pallas_call | solution.py:176
  66.4 48.3 %collective-permute-done.7.refs_0_ = bf16[1024,128]{1,0:T(8,128)(2,1)S(1)} collective-permute-done((bf16[1024,128]{1,0:T(8,128)(2,1)}, bf16[1024,128]{1,0:T(8,128)(2,1)S(1)}, u32[]{:S(2)}, u32[]{:S(2)}) %collective-permute-start.7) | collective-permute-done | bytes 262176 | tf_op jit(solution)/shard_map/ppermute | solution.py:246
  114.6 2.1 %shard_map.177 = (bf16[2048,512]{1,0:T(8,128)(2,1)}, bf16[2048,128]{1,0:T(8,128)(2,1)}, bf16[2048,128]{1,0:T(8,128)(2,1)}) custom-call(bf16[1024,128]{1,0:T(8,128)(2,1)S(1)} %collective-permute-done.7.refs_0_, bf16[1024,128]{1,0:T(8,128)(2,1)} %collective-permute-done.4.refs_1_, ...), custom_call_target="tpu_custom_call", output_to_operand_aliasing={{0}: (4, {}), {1}: (5, {}), {2}: (6, {})} | custom-call | tf_op jit(solution)/shard_map/pallas_call | solution.py:74
  116.7 2.2 %collective-permute-done.5.refs_0_ = bf16[1024,128]{1,0:T(8,128)(2,1)S(1)} collective-permute-done((bf16[1024,128]{1,0:T(8,128)(2,1)}, bf16[1024,128]{1,0:T(8,128)(2,1)S(1)}, u32[]{:S(2)}, u32[]{:S(2)}) %collective-permute-start.5) | collective-permute-done | bytes 262176 | tf_op jit(solution)/shard_map/ppermute | solution.py:246
  119.7 1.9 %shard_map.183 = bf16[512,2048]{1,0:T(8,128)(2,1)} custom-call(bf16[512,512]{1,0:T(8,128)(2,1)S(1)} %collective-permute-done.12.refs_0_, bf16[32,512]{1,0:T(8,128)(2,1)} %bitcast.16, bf16[640,128]{1,0:T(8,128)(2,1)S(1)} %pad_maximum_fusion.refs_3_.refs_2_, bf16[512,2048]{1,0:T(8,128)(2,1)} %shard_map.182.refs_3_), custom_call_target="tpu_custom_call", output_to_operand_aliasing={{}: (3, {})} | custom-call | tf_op jit(solution)/shard_map/pallas_call | solution.py:176
  (43 shorter events, 15.1 us)
Async XLA Ops:
  1.4 4.8 %collective-permute-start.13 = (bf16[40,128]{1,0:T(8,128)(2,1)S(1)}, bf16[40,128]{1,0:T(8,128)(2,1)S(1)}, u32[]{:S(2)}, u32[]{:S(2)}) collective-permute-start(bf16[40,128]{1,0:T(8,128)(2,1)S(1)} %shard_map.180), channel_id=1, source_target_pairs={{0,8},{8,0},{16,24},{24,16},{1,9},{9,1},{17,25},{25,17},{2,10},{10... | collective-permute-start | bytes 30728 | tf_op jit(solution)/shard_map/ppermute | solution.py:233
  6.2 6.4 %collective-permute-start.14 = (bf16[80,128]{1,0:T(8,128)(2,1)S(1)}, bf16[80,128]{1,0:T(8,128)(2,1)S(1)}, u32[]{:S(2)}, u32[]{:S(2)}) collective-permute-start(bf16[80,128]{1,0:T(8,128)(2,1)S(1)} %pad_maximum_fusion.3), channel_id=1, source_target_pairs={{0,16},{8,24},{16,0},{24,8},{1,17},{9,25},{17,1},{25,9},{2,18},{10... | collective-permute-start | bytes 61448 | tf_op jit(solution)/shard_map/ppermute | solution.py:233
  9.3 15.0 %collective-permute-start.10 = (bf16[512,512]{1,0:T(8,128)(2,1)}, bf16[512,512]{1,0:T(8,128)(2,1)S(1)}, u32[]{:S(2)}, u32[]{:S(2)}) collective-permute-start(bf16[512,512]{1,0:T(8,128)(2,1)} %refs_4_.1), channel_id=1, source_target_pairs={{0,8},{8,0},{16,24},{24,16},{1,9},{9,1},{17,25},{25,17},{2,10},{10... | collective-permute-start | bytes 1572872 | tf_op jit(solution)/shard_map/ppermute | solution.py:246
  12.1 23.4 %collective-permute-start = (bf16[512,512]{1,0:T(8,128)(2,1)S(1)}, bf16[512,512]{1,0:T(8,128)(2,1)S(1)}, u32[]{:S(2)}, u32[]{:S(2)}) collective-permute-start(bf16[512,512]{1,0:T(8,128)(2,1)S(1)} %shard_map.173.refs_1_), channel_id=1, source_target_pairs={{0,8},{8,0},{16,24},{24,16},{1,9},{9,1},{17,25},{25,17},{2,10},{10... | collective-permute-start | bytes 1572872 | tf_op jit(solution)/shard_map/ppermute | solution.py:246
  12.6 5.6 %collective-permute-start.15 = (bf16[160,128]{1,0:T(8,128)(2,1)S(1)}, bf16[160,128]{1,0:T(8,128)(2,1)S(1)}, u32[]{:S(2)}, u32[]{:S(2)}) collective-permute-start(bf16[160,128]{1,0:T(8,128)(2,1)S(1)} %pad_maximum_fusion.2), channel_id=1, source_target_pairs={{0,2},{2,0},{4,6},{6,4},{1,3},{3,1},{5,7},{7,5},{8,10},{10,8},{12,... | collective-permute-start | bytes 122888 | tf_op jit(solution)/shard_map/ppermute | solution.py:233
  12.7 26.9 %collective-permute-start.17 = (bf16[512,512]{1,0:T(8,128)(2,1)}, bf16[512,512]{1,0:T(8,128)(2,1)}, u32[]{:S(2)}, u32[]{:S(2)}) collective-permute-start(bf16[512,512]{1,0:T(8,128)(2,1)} %refs_4_.1), channel_id=1, source_target_pairs={{8,16},{16,8},{9,17},{17,9},{10,18},{18,10},{11,19},{19,11},{12,20... | collective-permute-start | bytes 1572872 | tf_op jit(solution)/shard_map/ppermute | solution.py:246
  15.6 23.3 %collective-permute-start.3 = (bf16[1024,128]{1,0:T(8,128)(2,1)S(1)}, bf16[1024,128]{1,0:T(8,128)(2,1)}, u32[]{:S(2)}, u32[]{:S(2)}) collective-permute-start(bf16[1024,128]{1,0:T(8,128)(2,1)S(1)} %shard_map.174.refs_0_), channel_id=1, source_target_pairs={{0,8},{8,0},{16,24},{24,16},{1,9},{9,1},{17,25},{25,17},{2,10},{10... | collective-permute-start | bytes 786440 | tf_op jit(solution)/shard_map/ppermute | solution.py:246
  18.2 4.6 %collective-permute-start.16 = (bf16[320,128]{1,0:T(8,128)(2,1)S(1)}, bf16[320,128]{1,0:T(8,128)(2,1)}, u32[]{:S(2)}, u32[]{:S(2)}) collective-permute-start(bf16[320,128]{1,0:T(8,128)(2,1)S(1)} %pad_maximum_fusion.1), channel_id=1, source_target_pairs={{0,4},{2,6},{4,0},{6,2},{1,5},{3,7},{5,1},{7,3},{8,12},{10,14},{12... | collective-permute-start | bytes 245768 | tf_op jit(solution)/shard_map/ppermute | solution.py:233
  22.9 19.4 %collective-permute-start.8 = (bf16[512,512]{1,0:T(8,128)(2,1)S(1)}, bf16[512,512]{1,0:T(8,128)(2,1)S(1)}, u32[]{:S(2)}, u32[]{:S(2)}) collective-permute-start(bf16[512,512]{1,0:T(8,128)(2,1)S(1)} %shard_map.173.refs_1_), channel_id=1, source_target_pairs={{8,16},{16,8},{9,17},{17,9},{10,18},{18,10},{11,19},{19,11},{12,20... | collective-permute-start | bytes 1572872 | tf_op jit(solution)/shard_map/ppermute | solution.py:246
  24.3 19.3 %collective-permute-start.11 = (bf16[512,512]{1,0:T(8,128)(2,1)S(1)}, bf16[512,512]{1,0:T(8,128)(2,1)}, u32[]{:S(2)}, u32[]{:S(2)}) collective-permute-start(bf16[512,512]{1,0:T(8,128)(2,1)S(1)} %collective-permute-done.10.refs_0_), channel_id=1, source_target_pairs={{8,16},{16,8},{9,17},{17,9},{10,18},{18,10},{11,19},{19,11},{12,20... | collective-permute-start | bytes 1572872 | tf_op jit(solution)/shard_map/ppermute | solution.py:246
  25.8 0.8 copy-start
  35.5 9.4 %collective-permute-start.1 = (bf16[512,512]{1,0:T(8,128)(2,1)S(1)}, bf16[512,512]{1,0:T(8,128)(2,1)S(1)}, u32[]{:S(2)}, u32[]{:S(2)}) collective-permute-start(bf16[512,512]{1,0:T(8,128)(2,1)S(1)} %collective-permute-done.refs_2_), channel_id=1, source_target_pairs={{8,16},{16,8},{9,17},{17,9},{10,18},{18,10},{11,19},{19,11},{12,20... | collective-permute-start | bytes 1572872 | tf_op jit(solution)/shard_map/ppermute | solution.py:246
  38.9 2.0 %collective-permute-start.6 = (bf16[1024,128]{1,0:T(8,128)(2,1)S(1)}, bf16[1024,128]{1,0:T(8,128)(2,1)S(1)}, u32[]{:S(2)}, u32[]{:S(2)}) collective-permute-start(bf16[1024,128]{1,0:T(8,128)(2,1)S(1)} %shard_map.174.refs_0_), channel_id=1, source_target_pairs={{8,16},{16,8},{9,17},{17,9},{10,18},{18,10},{11,19},{19,11},{12,20... | collective-permute-start | bytes 786440 | tf_op jit(solution)/shard_map/ppermute | solution.py:246
  39.6 14.3 %collective-permute-start.18 = (bf16[512,512]{1,0:T(8,128)(2,1)}, bf16[512,512]{1,0:T(8,128)(2,1)}, u32[]{:S(2)}, u32[]{:S(2)}) collective-permute-start(bf16[512,512]{1,0:T(8,128)(2,1)} %collective-permute-done.17.refs_1_), channel_id=1, source_target_pairs={{8,0},{16,24},{9,1},{17,25},{10,2},{18,26},{11,3},{19,27},{12,4},{... | collective-permute-start | bytes 1572872 | tf_op jit(solution)/shard_map/ppermute | solution.py:246
  40.9 2.7 %copy-start.2 = (bf16[1024,128]{1,0:T(8,128)(2,1)}, bf16[1024,128]{1,0:T(8,128)(2,1)S(1)}, u32[]{:S(2)}) copy-start(bf16[1024,128]{1,0:T(8,128)(2,1)S(1)} %collective-permute-done.6.refs_1_) | copy-start | bytes 786436
  40.9 6.3 %collective-permute-start.4 = (bf16[1024,128]{1,0:T(8,128)(2,1)}, bf16[1024,128]{1,0:T(8,128)(2,1)}, u32[]{:S(2)}, u32[]{:S(2)}) collective-permute-start(bf16[1024,128]{1,0:T(8,128)(2,1)} %collective-permute-done.3.refs_0_), channel_id=1, source_target_pairs={{8,16},{16,8},{9,17},{17,9},{10,18},{18,10},{11,19},{19,11},{12,20... | collective-permute-start | bytes 786440 | tf_op jit(solution)/shard_map/ppermute | solution.py:246
  42.3 72.4 %collective-permute-start.9 = (bf16[512,512]{1,0:T(8,128)(2,1)S(1)}, bf16[512,512]{1,0:T(8,128)(2,1)}, u32[]{:S(2)}, u32[]{:S(2)}) collective-permute-start(bf16[512,512]{1,0:T(8,128)(2,1)S(1)} %collective-permute-done.8.refs_3_), channel_id=1, source_target_pairs={{8,0},{16,24},{9,1},{17,25},{10,2},{18,26},{11,3},{19,27},{12,4},{... | collective-permute-start | bytes 1572872 | tf_op jit(solution)/shard_map/ppermute | solution.py:246
  43.6 76.0 %collective-permute-start.12 = (bf16[512,512]{1,0:T(8,128)(2,1)}, bf16[512,512]{1,0:T(8,128)(2,1)S(1)}, u32[]{:S(2)}, u32[]{:S(2)}) collective-permute-start(bf16[512,512]{1,0:T(8,128)(2,1)} %collective-permute-done.11.refs_1_), channel_id=1, source_target_pairs={{8,0},{16,24},{9,1},{17,25},{10,2},{18,26},{11,3},{19,27},{12,4},{... | collective-permute-start | bytes 1572872 | tf_op jit(solution)/shard_map/ppermute | solution.py:246
  44.9 76.7 %collective-permute-start.2 = (bf16[512,512]{1,0:T(8,128)(2,1)S(1)}, bf16[512,512]{1,0:T(8,128)(2,1)S(1)}, u32[]{:S(2)}, u32[]{:S(2)}) collective-permute-start(bf16[512,512]{1,0:T(8,128)(2,1)S(1)} %collective-permute-done.1.refs_3_), channel_id=1, source_target_pairs={{8,0},{16,24},{9,1},{17,25},{10,2},{18,26},{11,3},{19,27},{12,4},{... | collective-permute-start | bytes 1572872 | tf_op jit(solution)/shard_map/ppermute | solution.py:246
  47.2 67.5 %collective-permute-start.7 = (bf16[1024,128]{1,0:T(8,128)(2,1)}, bf16[1024,128]{1,0:T(8,128)(2,1)S(1)}, u32[]{:S(2)}, u32[]{:S(2)}) collective-permute-start(bf16[1024,128]{1,0:T(8,128)(2,1)} %copy-done.2), channel_id=1, source_target_pairs={{8,0},{16,24},{9,1},{17,25},{10,2},{18,26},{11,3},{19,27},{12,4},{... | collective-permute-start | bytes 786440 | tf_op jit(solution)/shard_map/ppermute | solution.py:246
  53.8 65.1 %collective-permute-start.5 = (bf16[1024,128]{1,0:T(8,128)(2,1)}, bf16[1024,128]{1,0:T(8,128)(2,1)S(1)}, u32[]{:S(2)}, u32[]{:S(2)}) collective-permute-start(bf16[1024,128]{1,0:T(8,128)(2,1)} %collective-permute-done.4.refs_1_), channel_id=1, source_target_pairs={{8,0},{16,24},{9,1},{17,25},{10,2},{18,26},{11,3},{19,27},{12,4},{... | collective-permute-start | bytes 786440 | tf_op jit(solution)/shard_map/ppermute | solution.py:246
  56.1 5.3 %copy-start.3 = (bf16[1024,128]{1,0:T(8,128)(2,1)S(1)}, bf16[1024,128]{1,0:T(8,128)(2,1)}, u32[]{:S(2)}) copy-start(bf16[1024,128]{1,0:T(8,128)(2,1)} %copy-done.2) | copy-start | bytes 786436
  56.7 1.0 copy-start.1

commit v3 on v2

--- a/solution.py
+++ b/solution.py
@@ -242,15 +242,24 @@
                 fresh = [None, None]
                 for side in (0, 1):
                     pairs = live(side, step)
-                    if pairs:
+
+                    def shard(i, side=side, step=step):
+                        return source(i, side, step)
+
+                    def there(i, side=side, step=step):
+                        return (source(i, side, step) >= 0) & (source(i, side, step) < zeros)
+
+                    if pairs and step == zeros - 1 and c == 2 and models % 2 == 0:
+                        for half in (0, 1):
+                            both = [(a * models + m, b * models + m) for a, b in pairs for m in range(half, models, 2)]
+                            part = lax.ppermute(held[c][1 - side], ("zero", "model"), both)
+
+                            def mine(i, there=there, half=half):
+                                return there(i) & (lax.axis_index("model") % 2 == half)
+
+                            arrived.append((part, kinds[c], shard, mine))
+                    elif pairs:
                         fresh[side] = lax.ppermute(held[c][1 - side], "zero", pairs)
-
-                        def shard(i, side=side, step=step):
-                            return source(i, side, step)
-
-                        def there(i, side=side, step=step):
-                            return (source(i, side, step) >= 0) & (source(i, side, step) < zeros)
-
                         if c == 0:
                             raw.append((fresh[side], shard, there))
                         else:

time: 123 us -> 128 us (1.041)
  local copies, waits for them, and re-layouts: 2.45 us -> 4.54 us
    unnamed x8 -> x22, local copies, waits for them, and re-layouts: 1.84 us -> 3.94 us
    ppermute x0 -> x2, starting transfers between devices: none -> 1.97 us  [shards(): part = lax.ppermute(held[c][1 - side], ('zero', 'model'), both)]
    pallas_call x5 -> x6, Pallas kernels: 6.45 us -> 5.48 us  [place(): pl.pallas_call(body, in_specs=[pl.BlockSpec(memory_space=pltpu.VMEM)] * l...]
    ppermute x15 -> x14, waiting for transfers between devices: 68.3 us -> 69.2 us  [shards(): fresh[side] = lax.ppermute(held[c][1 - side], 'zero', pairs)]
    ppermute x15 -> x14, starting transfers between devices: 18.8 us -> 17.9 us  [shards(): fresh[side] = lax.ppermute(held[c][1 - side], 'zero', pairs)]
  transfers between devices with their start and end apart: 19 -> 20, of which waited for: 8 -> 7; matrix products, arithmetic and copies ran while one was open for 1% -> 1% of each run, Pallas kernels for 14% -> 14%
where the time goes in v3:
time: 128 us; the launch traced here: 127 us
  waiting for transfers between devices  74.1 us (58%)
  starting transfers between devices  27.7 us (22%)
  Pallas kernels  18.5 us (14%)
  local copies, waits for them, and re-layouts  4.54 us (4%)
    ppermute x14, waiting for transfers between devices, shards(): fresh[side] = lax.ppermute(held[c][1 - side], 'zero', pairs)  69.2 us
    ppermute x14, starting transfers between devices, shards(): fresh[side] = lax.ppermute(held[c][1 - side], 'zero', pairs)  17.9 us
    pallas_call x3, Pallas kernels, finish(): pl.pallas_call(body, in_specs=[pl.BlockSpec(memory_space=pltpu.VMEM)] * l...  9.68 us
    ppermute x4, starting transfers between devices, shards(): other = lax.ppermute(shared, axis, [(i, i ^ hop) for i in range(size)])  7.85 us
    pallas_call x6, Pallas kernels, place(): pl.pallas_call(body, in_specs=[pl.BlockSpec(memory_space=pltpu.VMEM)] * l...  5.48 us
    ppermute x4, waiting for transfers between devices, shards(): other = lax.ppermute(shared, axis, [(i, i ^ hop) for i in range(size)])  4.9 us
    unnamed x22, local copies, waits for them, and re-layouts  3.94 us
    pallas_call x2, Pallas kernels, merge(): pl.pallas_call(body, in_specs=[pl.BlockSpec(memory_space=pltpu.HBM)] * le...  2.59 us
  transfers between devices with their start and end apart: 20, of which 7 were waited for; matrix products, arithmetic and copies ran while one was open for 1% of the time, Pallas kernels for 14%

profile of v3, /device:TPU:0, one launch (start us, length us, event | category | flops | bytes accessed | tf_op | source)
XLA Modules:
  0.0 126.9 jit_solution(2160332358382153588)
XLA Ops:
  1.4 3.1 %collective-permute-start.14 = (bf16[40,128]{1,0:T(8,128)(2,1)S(1)}, bf16[40,128]{1,0:T(8,128)(2,1)S(1)}, u32[]{:S(2)}, u32[]{:S(2)}) collective-permute-start(bf16[40,128]{1,0:T(8,128)(2,1)S(1)} %shard_map.181), channel_id=1, source_target_pairs={{0,8},{8,0},{16,24},{24,16},{1,9},{9,1},{17,25},{25,17},{2,10},{10... | collective-permute-start | bytes 30728 | tf_op jit(solution)/shard_map/ppermute | solution.py:233
  4.5 1.7 %collective-permute-done.14 = bf16[40,128]{1,0:T(8,128)(2,1)S(1)} collective-permute-done((bf16[40,128]{1,0:T(8,128)(2,1)S(1)}, bf16[40,128]{1,0:T(8,128)(2,1)S(1)}, u32[]{:S(2)}, u32[]{:S(2)}) %collective-permute-start.14) | collective-permute-done | bytes 10272 | tf_op jit(solution)/shard_map/ppermute | solution.py:233
  6.2 3.1 %collective-permute-start.15 = (bf16[80,128]{1,0:T(8,128)(2,1)S(1)}, bf16[80,128]{1,0:T(8,128)(2,1)S(1)}, u32[]{:S(2)}, u32[]{:S(2)}) collective-permute-start(bf16[80,128]{1,0:T(8,128)(2,1)S(1)} %pad_maximum_fusion.3), channel_id=1, source_target_pairs={{0,16},{8,24},{16,0},{24,8},{1,17},{9,25},{17,1},{25,9},{2,18},{10... | collective-permute-start | bytes 61448 | tf_op jit(solution)/shard_map/ppermute | solution.py:233
  9.3 1.8 %collective-permute-done.15 = bf16[80,128]{1,0:T(8,128)(2,1)S(1)} collective-permute-done((bf16[80,128]{1,0:T(8,128)(2,1)S(1)}, bf16[80,128]{1,0:T(8,128)(2,1)S(1)}, u32[]{:S(2)}, u32[]{:S(2)}) %collective-permute-start.15) | collective-permute-done | bytes 20512 | tf_op jit(solution)/shard_map/ppermute | solution.py:233
  11.1 2.0 %collective-permute-start.11 = (bf16[512,512]{1,0:T(8,128)(2,1)}, bf16[512,512]{1,0:T(8,128)(2,1)S(1)}, u32[]{:S(2)}, u32[]{:S(2)}) collective-permute-start(bf16[512,512]{1,0:T(8,128)(2,1)} %refs_4_.1), channel_id=1, source_target_pairs={{0,8},{8,0},{16,24},{24,16},{1,9},{9,1},{17,25},{25,17},{2,10},{10... | collective-permute-start | bytes 1572872 | tf_op jit(solution)/shard_map/ppermute | solution.py:262
  13.1 1.5 %collective-permute-start.18 = (bf16[512,512]{1,0:T(8,128)(2,1)}, bf16[512,512]{1,0:T(8,128)(2,1)}, u32[]{:S(2)}, u32[]{:S(2)}) collective-permute-start(bf16[512,512]{1,0:T(8,128)(2,1)} %refs_4_.1), channel_id=1, source_target_pairs={{8,16},{16,8},{9,17},{17,9},{10,18},{18,10},{11,19},{19,11},{12,20... | collective-permute-start | bytes 1572872 | tf_op jit(solution)/shard_map/ppermute | solution.py:262
  15.8 3.8 %collective-permute-start = (bf16[512,512]{1,0:T(8,128)(2,1)S(1)}, bf16[512,512]{1,0:T(8,128)(2,1)S(1)}, u32[]{:S(2)}, u32[]{:S(2)}) collective-permute-start(bf16[512,512]{1,0:T(8,128)(2,1)S(1)} %shard_map.173.refs_1_), channel_id=1, source_target_pairs={{0,8},{8,0},{16,24},{24,16},{1,9},{9,1},{17,25},{25,17},{2,10},{10... | collective-permute-start | bytes 1572872 | tf_op jit(solution)/shard_map/ppermute | solution.py:262
  19.6 1.6 %collective-permute-start.17 = (bf16[320,128]{1,0:T(8,128)(2,1)S(1)}, bf16[320,128]{1,0:T(8,128)(2,1)S(1)}, u32[]{:S(2)}, u32[]{:S(2)}) collective-permute-start(bf16[320,128]{1,0:T(8,128)(2,1)S(1)} %pad_maximum_fusion.1), channel_id=1, source_target_pairs={{0,4},{2,6},{4,0},{6,2},{1,5},{3,7},{5,1},{7,3},{8,12},{10,14},{12... | collective-permute-start | bytes 245768 | tf_op jit(solution)/shard_map/ppermute | solution.py:233
  21.2 1.4 %shard_map.174.refs_0_ = bf16[1024,128]{1,0:T(8,128)(2,1)S(1)} custom-call(bf16[512,128]{1,0:T(8,128)(2,1)} %refs_0_.3, bf16[32,512]{1,0:T(8,128)(2,1)} %bitcast.18, bf16[32,128]{1,0:T(8,128)(2,1)} %refs_2_.3, bf16[512,128]{1,0:T(8,128)(2,1)} %refs_3_.1, bf16[32,512]{1,0:T(8,128)(2,1)} %bitcast.19, bf16[32,128]{1,0:T(8,128)(2,1)} %refs_5_.1), custom_call_target="tpu_custom_call" | custom-call | tf_op jit(solution)/shard_map/pallas_call | solution.py:40
  22.7 1.5 %collective-permute-done.17 = bf16[320,128]{1,0:T(8,128)(2,1)S(1)} collective-permute-done((bf16[320,128]{1,0:T(8,128)(2,1)S(1)}, bf16[320,128]{1,0:T(8,128)(2,1)S(1)}, u32[]{:S(2)}, u32[]{:S(2)}) %collective-permute-start.17) | collective-permute-done | bytes 81952 | tf_op jit(solution)/shard_map/ppermute | solution.py:233
  24.8 17.9 %collective-permute-done.4.refs_0_ = bf16[1024,128]{1,0:T(8,128)(2,1)S(1)} collective-permute-done((bf16[1024,128]{1,0:T(8,128)(2,1)S(1)}, bf16[1024,128]{1,0:T(8,128)(2,1)S(1)}, u32[]{:S(2)}, u32[]{:S(2)}) %collective-permute-start.4) | collective-permute-done | bytes 262176 | tf_op jit(solution)/shard_map/ppermute | solution.py:262
  43.4 1.5 %collective-permute-start.12 = (bf16[512,512]{1,0:T(8,128)(2,1)S(1)}, bf16[512,512]{1,0:T(8,128)(2,1)}, u32[]{:S(2)}, u32[]{:S(2)}) collective-permute-start(bf16[512,512]{1,0:T(8,128)(2,1)S(1)} %collective-permute-done.11.refs_0_), channel_id=1, source_target_pairs={{8,16},{16,8},{9,17},{17,9},{10,18},{18,10},{11,19},{19,11},{12,20... | collective-permute-start | bytes 1572872 | tf_op jit(solution)/shard_map/ppermute | solution.py:262
  46.3 1.3 %collective-permute-start.19 = (bf16[512,512]{1,0:T(8,128)(2,1)}, bf16[512,512]{1,0:T(8,128)(2,1)}, u32[]{:S(2)}, u32[]{:S(2)}) collective-permute-start(bf16[512,512]{1,0:T(8,128)(2,1)} %collective-permute-done.18.refs_1_), channel_id=1, source_target_pairs={{8,0},{16,24},{9,1},{17,25},{10,2},{18,26},{11,3},{19,27},{12,4},{... | collective-permute-start | bytes 1572872 | tf_op jit(solution)/shard_map/ppermute | solution.py:262
  49.1 1.3 %collective-permute-start.8 = (bf16[1024,128]{1,0:T(8,128)(2,1)S(1)}, bf16[1024,128]{1,0:T(8,128)(2,1)S(1)}, u32[]{:S(2)}, u32[]{:S(2)}) collective-permute-start(bf16[1024,128]{1,0:T(8,128)(2,1)S(1)} %collective-permute-done.7.refs_1_), channel_id=1, source_target_pairs={{8,0},{16,24},{9,1},{17,25},{10,2},{18,26},{11,3},{19,27},{12,4},{... | collective-permute-start | bytes 786440 | tf_op jit(solution)/shard_map/ppermute | solution.py:262
  52.4 1.3 %collective-permute-start.13 = (bf16[512,512]{1,0:T(8,128)(2,1)}, bf16[512,512]{1,0:T(8,128)(2,1)}, u32[]{:S(2)}, u32[]{:S(2)}) collective-permute-start(bf16[512,512]{1,0:T(8,128)(2,1)} %collective-permute-done.12.refs_1_), channel_id=1, source_target_pairs={{8,0},{16,24},{9,1},{17,25},{10,2},{18,26},{11,3},{19,27},{12,4},{... | collective-permute-start | bytes 1572872 | tf_op jit(solution)/shard_map/ppermute | solution.py:262
  53.7 1.3 %collective-permute-start.3 = (bf16[512,512]{1,0:T(8,128)(2,1)S(1)}, bf16[512,512]{1,0:T(8,128)(2,1)S(1)}, u32[]{:S(2)}, u32[]{:S(2)}) collective-permute-start(bf16[512,512]{1,0:T(8,128)(2,1)S(1)} %collective-permute-done.1.refs_3_), channel_id=1, source_target_pairs={{8,0},{12,4},{16,24},{20,28},{9,1},{13,5},{17,25},{21,29}} | collective-permute-start | bytes 1572872 | tf_op jit(solution)/shard_map/ppermute | solution.py:255
  55.0 17.5 %collective-permute-done.8.refs_0_ = bf16[1024,128]{1,0:T(8,128)(2,1)S(1)} collective-permute-done((bf16[1024,128]{1,0:T(8,128)(2,1)S(1)}, bf16[1024,128]{1,0:T(8,128)(2,1)S(1)}, u32[]{:S(2)}, u32[]{:S(2)}) %collective-permute-start.8) | collective-permute-done | bytes 262176 | tf_op jit(solution)/shard_map/ppermute | solution.py:262
  74.9 1.3 %collective-permute-start.6 = (bf16[1024,128]{1,0:T(8,128)(2,1)}, bf16[1024,128]{1,0:T(8,128)(2,1)S(1)}, u32[]{:S(2)}, u32[]{:S(2)}) collective-permute-start(bf16[1024,128]{1,0:T(8,128)(2,1)} %copy-done.6), channel_id=1, source_target_pairs={{8,0},{16,24},{9,1},{17,25},{10,2},{18,26},{11,3},{19,27},{12,4},{... | collective-permute-start | bytes 786440 | tf_op jit(solution)/shard_map/ppermute | solution.py:262
  78.8 3.6 %shard_map.182.refs_4_ = bf16[512,2048]{1,0:T(8,128)(2,1)} custom-call(bf16[512,512]{1,0:T(8,128)(2,1)S(1)} %copy-done.1, bf16[512,512]{1,0:T(8,128)(2,1)} %collective-permute-done.18.refs_1_, bf16[32,512]{1,0:T(8,128)(2,1)} %bitcast.14, bf16[640,128]{1,0:T(8,128)(2,1)S(1)} %pad_maximum_fusion.refs_3_.refs_2_, bf16[512,512]{1,0:T(8,128)(2,1)} %refs_4_.1), custom_call_target="tpu_custom_call" | custom-call | tf_op jit(solution)/shard_map/pallas_call | solution.py:176
  83.4 3.2 %shard_map.183.refs_3_ = bf16[512,2048]{1,0:T(8,128)(2,1)} custom-call(bf16[512,512]{1,0:T(8,128)(2,1)} %collective-permute-done.19.refs_0_, bf16[512,512]{1,0:T(8,128)(2,1)} %collective-permute-done.12.refs_1_, bf16[32,512]{1,0:T(8,128)(2,1)} %bitcast.15, bf16[640,128]{1,0:T(8,128)(2,1)S(1)} %pad_maximum_fusion.refs_3_.refs_2_, ...), custom_call_target="tpu_custom_call", output_to_operand_aliasing={{}: (4, {})} | custom-call | tf_op jit(solution)/shard_map/pallas_call | solution.py:176
  86.6 9.7 %collective-permute-done.10.refs_2_ = bf16[512,512]{1,0:T(8,128)(2,1)} collective-permute-done((bf16[512,512]{1,0:T(8,128)(2,1)S(1)}, bf16[512,512]{1,0:T(8,128)(2,1)}, u32[]{:S(2)}, u32[]{:S(2)}) %collective-permute-start.10) | collective-permute-done | bytes 524320 | tf_op jit(solution)/shard_map/ppermute | solution.py:262
  96.3 2.0 %shard_map.177 = (bf16[2048,512]{1,0:T(8,128)(2,1)}, bf16[2048,128]{1,0:T(8,128)(2,1)}, bf16[2048,128]{1,0:T(8,128)(2,1)}) custom-call(bf16[1024,128]{1,0:T(8,128)(2,1)S(1)} %copy-done.9, bf16[1024,128]{1,0:T(8,128)(2,1)S(1)} %copy-done.7, ...), custom_call_target="tpu_custom_call", output_to_operand_aliasing={{0}: (4, {}), {1}: (5, {}), {2}: (6, {})} | custom-call | tf_op jit(solution)/shard_map/pallas_call | solution.py:74
  98.3 24.0 %collective-permute-done.6.refs_0_ = bf16[1024,128]{1,0:T(8,128)(2,1)S(1)} collective-permute-done((bf16[1024,128]{1,0:T(8,128)(2,1)}, bf16[1024,128]{1,0:T(8,128)(2,1)S(1)}, u32[]{:S(2)}, u32[]{:S(2)}) %collective-permute-start.6) | collective-permute-done | bytes 262176 | tf_op jit(solution)/shard_map/ppermute | solution.py:262
  123.1 2.9 %shard_map.184 = bf16[512,2048]{1,0:T(8,128)(2,1)} custom-call(bf16[512,512]{1,0:T(8,128)(2,1)} %collective-permute-done.13.refs_0_, bf16[32,512]{1,0:T(8,128)(2,1)} %bitcast.16, bf16[640,128]{1,0:T(8,128)(2,1)S(1)} %pad_maximum_fusion.refs_3_.refs_2_, bf16[512,2048]{1,0:T(8,128)(2,1)} %shard_map.183.refs_3_), custom_call_target="tpu_custom_call", output_to_operand_aliasing={{}: (3, {})} | custom-call | tf_op jit(solution)/shard_map/pallas_call | solution.py:176
  (60 shorter events, 15.9 us)
Async XLA Ops:
  1.4 4.8 %collective-permute-start.14 = (bf16[40,128]{1,0:T(8,128)(2,1)S(1)}, bf16[40,128]{1,0:T(8,128)(2,1)S(1)}, u32[]{:S(2)}, u32[]{:S(2)}) collective-permute-start(bf16[40,128]{1,0:T(8,128)(2,1)S(1)} %shard_map.181), channel_id=1, source_target_pairs={{0,8},{8,0},{16,24},{24,16},{1,9},{9,1},{17,25},{25,17},{2,10},{10... | collective-permute-start | bytes 30728 | tf_op jit(solution)/shard_map/ppermute | solution.py:233
  6.2 4.9 %collective-permute-start.15 = (bf16[80,128]{1,0:T(8,128)(2,1)S(1)}, bf16[80,128]{1,0:T(8,128)(2,1)S(1)}, u32[]{:S(2)}, u32[]{:S(2)}) collective-permute-start(bf16[80,128]{1,0:T(8,128)(2,1)S(1)} %pad_maximum_fusion.3), channel_id=1, source_target_pairs={{0,16},{8,24},{16,0},{24,8},{1,17},{9,25},{17,1},{25,9},{2,18},{10... | collective-permute-start | bytes 61448 | tf_op jit(solution)/shard_map/ppermute | solution.py:233
  11.1 8.5 %collective-permute-start.16 = (bf16[160,128]{1,0:T(8,128)(2,1)S(1)}, bf16[160,128]{1,0:T(8,128)(2,1)S(1)}, u32[]{:S(2)}, u32[]{:S(2)}) collective-permute-start(bf16[160,128]{1,0:T(8,128)(2,1)S(1)} %pad_maximum_fusion.2), channel_id=1, source_target_pairs={{0,2},{2,0},{4,6},{6,4},{1,3},{3,1},{5,7},{7,5},{8,10},{10,8},{12,... | collective-permute-start | bytes 122888 | tf_op jit(solution)/shard_map/ppermute | solution.py:233
  11.1 32.2 %collective-permute-start.11 = (bf16[512,512]{1,0:T(8,128)(2,1)}, bf16[512,512]{1,0:T(8,128)(2,1)S(1)}, u32[]{:S(2)}, u32[]{:S(2)}) collective-permute-start(bf16[512,512]{1,0:T(8,128)(2,1)} %refs_4_.1), channel_id=1, source_target_pairs={{0,8},{8,0},{16,24},{24,16},{1,9},{9,1},{17,25},{25,17},{2,10},{10... | collective-permute-start | bytes 1572872 | tf_op jit(solution)/shard_map/ppermute | solution.py:262
  13.1 33.2 %collective-permute-start.18 = (bf16[512,512]{1,0:T(8,128)(2,1)}, bf16[512,512]{1,0:T(8,128)(2,1)}, u32[]{:S(2)}, u32[]{:S(2)}) collective-permute-start(bf16[512,512]{1,0:T(8,128)(2,1)} %refs_4_.1), channel_id=1, source_target_pairs={{8,16},{16,8},{9,17},{17,9},{10,18},{18,10},{11,19},{19,11},{12,20... | collective-permute-start | bytes 1572872 | tf_op jit(solution)/shard_map/ppermute | solution.py:262
  15.8 29.8 %collective-permute-start = (bf16[512,512]{1,0:T(8,128)(2,1)S(1)}, bf16[512,512]{1,0:T(8,128)(2,1)S(1)}, u32[]{:S(2)}, u32[]{:S(2)}) collective-permute-start(bf16[512,512]{1,0:T(8,128)(2,1)S(1)} %shard_map.173.refs_1_), channel_id=1, source_target_pairs={{0,8},{8,0},{16,24},{24,16},{1,9},{9,1},{17,25},{25,17},{2,10},{10... | collective-permute-start | bytes 1572872 | tf_op jit(solution)/shard_map/ppermute | solution.py:262
  19.6 4.5 %collective-permute-start.17 = (bf16[320,128]{1,0:T(8,128)(2,1)S(1)}, bf16[320,128]{1,0:T(8,128)(2,1)S(1)}, u32[]{:S(2)}, u32[]{:S(2)}) collective-permute-start(bf16[320,128]{1,0:T(8,128)(2,1)S(1)} %pad_maximum_fusion.1), channel_id=1, source_target_pairs={{0,4},{2,6},{4,0},{6,2},{1,5},{3,7},{5,1},{7,3},{8,12},{10,14},{12... | collective-permute-start | bytes 245768 | tf_op jit(solution)/shard_map/ppermute | solution.py:233
  22.6 20.1 %collective-permute-start.4 = (bf16[1024,128]{1,0:T(8,128)(2,1)S(1)}, bf16[1024,128]{1,0:T(8,128)(2,1)S(1)}, u32[]{:S(2)}, u32[]{:S(2)}) collective-permute-start(bf16[1024,128]{1,0:T(8,128)(2,1)S(1)} %shard_map.174.refs_0_), channel_id=1, source_target_pairs={{0,8},{8,0},{16,24},{24,16},{1,9},{9,1},{17,25},{25,17},{2,10},{10... | collective-permute-start | bytes 786440 | tf_op jit(solution)/shard_map/ppermute | solution.py:262
  24.1 23.5 %copy-start.10 = (bf16[320,128]{1,0:T(8,128)(2,1)}, bf16[320,128]{1,0:T(8,128)(2,1)S(1)}, u32[]{:S(2)}) copy-start(bf16[320,128]{1,0:T(8,128)(2,1)S(1)} %collective-permute-done.17) | copy-start | bytes 245764
  24.1 24.9 %collective-permute-start.9 = (bf16[512,512]{1,0:T(8,128)(2,1)S(1)}, bf16[512,512]{1,0:T(8,128)(2,1)S(1)}, u32[]{:S(2)}, u32[]{:S(2)}) collective-permute-start(bf16[512,512]{1,0:T(8,128)(2,1)S(1)} %shard_map.173.refs_1_), channel_id=1, source_target_pairs={{8,16},{16,8},{9,17},{17,9},{10,18},{18,10},{11,19},{19,11},{12,20... | collective-permute-start | bytes 1572872 | tf_op jit(solution)/shard_map/ppermute | solution.py:262
  42.7 5.0 %collective-permute-start.7 = (bf16[1024,128]{1,0:T(8,128)(2,1)S(1)}, bf16[1024,128]{1,0:T(8,128)(2,1)S(1)}, u32[]{:S(2)}, u32[]{:S(2)}) collective-permute-start(bf16[1024,128]{1,0:T(8,128)(2,1)S(1)} %shard_map.174.refs_0_), channel_id=1, source_target_pairs={{8,16},{16,8},{9,17},{17,9},{10,18},{18,10},{11,19},{19,11},{12,20... | collective-permute-start | bytes 786440 | tf_op jit(solution)/shard_map/ppermute | solution.py:262
  43.4 9.0 %collective-permute-start.12 = (bf16[512,512]{1,0:T(8,128)(2,1)S(1)}, bf16[512,512]{1,0:T(8,128)(2,1)}, u32[]{:S(2)}, u32[]{:S(2)}) collective-permute-start(bf16[512,512]{1,0:T(8,128)(2,1)S(1)} %collective-permute-done.11.refs_0_), channel_id=1, source_target_pairs={{8,16},{16,8},{9,17},{17,9},{10,18},{18,10},{11,19},{19,11},{12,20... | collective-permute-start | bytes 1572872 | tf_op jit(solution)/shard_map/ppermute | solution.py:262
  45.6 8.0 %collective-permute-start.1 = (bf16[512,512]{1,0:T(8,128)(2,1)S(1)}, bf16[512,512]{1,0:T(8,128)(2,1)S(1)}, u32[]{:S(2)}, u32[]{:S(2)}) collective-permute-start(bf16[512,512]{1,0:T(8,128)(2,1)S(1)} %collective-permute-done.refs_2_), channel_id=1, source_target_pairs={{8,16},{16,8},{9,17},{17,9},{10,18},{18,10},{11,19},{19,11},{12,20... | collective-permute-start | bytes 1572872 | tf_op jit(solution)/shard_map/ppermute | solution.py:262
  46.3 28.5 %collective-permute-start.19 = (bf16[512,512]{1,0:T(8,128)(2,1)}, bf16[512,512]{1,0:T(8,128)(2,1)}, u32[]{:S(2)}, u32[]{:S(2)}) collective-permute-start(bf16[512,512]{1,0:T(8,128)(2,1)} %collective-permute-done.18.refs_1_), channel_id=1, source_target_pairs={{8,0},{16,24},{9,1},{17,25},{10,2},{18,26},{11,3},{19,27},{12,4},{... | collective-permute-start | bytes 1572872 | tf_op jit(solution)/shard_map/ppermute | solution.py:262
  47.7 3.4 %collective-permute-start.5 = (bf16[1024,128]{1,0:T(8,128)(2,1)S(1)}, bf16[1024,128]{1,0:T(8,128)(2,1)S(1)}, u32[]{:S(2)}, u32[]{:S(2)}) collective-permute-start(bf16[1024,128]{1,0:T(8,128)(2,1)S(1)} %collective-permute-done.4.refs_0_), channel_id=1, source_target_pairs={{8,16},{16,8},{9,17},{17,9},{10,18},{18,10},{11,19},{19,11},{12,20... | collective-permute-start | bytes 786440 | tf_op jit(solution)/shard_map/ppermute | solution.py:262
  49.1 23.5 %collective-permute-start.8 = (bf16[1024,128]{1,0:T(8,128)(2,1)S(1)}, bf16[1024,128]{1,0:T(8,128)(2,1)S(1)}, u32[]{:S(2)}, u32[]{:S(2)}) collective-permute-start(bf16[1024,128]{1,0:T(8,128)(2,1)S(1)} %collective-permute-done.7.refs_1_), channel_id=1, source_target_pairs={{8,0},{16,24},{9,1},{17,25},{10,2},{18,26},{11,3},{19,27},{12,4},{... | collective-permute-start | bytes 786440 | tf_op jit(solution)/shard_map/ppermute | solution.py:262
  51.1 45.3 %collective-permute-start.10 = (bf16[512,512]{1,0:T(8,128)(2,1)S(1)}, bf16[512,512]{1,0:T(8,128)(2,1)}, u32[]{:S(2)}, u32[]{:S(2)}) collective-permute-start(bf16[512,512]{1,0:T(8,128)(2,1)S(1)} %collective-permute-done.9.refs_3_), channel_id=1, source_target_pairs={{8,0},{16,24},{9,1},{17,25},{10,2},{18,26},{11,3},{19,27},{12,4},{... | collective-permute-start | bytes 1572872 | tf_op jit(solution)/shard_map/ppermute | solution.py:262
  52.4 70.7 %collective-permute-start.13 = (bf16[512,512]{1,0:T(8,128)(2,1)}, bf16[512,512]{1,0:T(8,128)(2,1)}, u32[]{:S(2)}, u32[]{:S(2)}) collective-permute-start(bf16[512,512]{1,0:T(8,128)(2,1)} %collective-permute-done.12.refs_1_), channel_id=1, source_target_pairs={{8,0},{16,24},{9,1},{17,25},{10,2},{18,26},{11,3},{19,27},{12,4},{... | collective-permute-start | bytes 1572872 | tf_op jit(solution)/shard_map/ppermute | solution.py:262
  53.7 72.4 %collective-permute-start.3 = (bf16[512,512]{1,0:T(8,128)(2,1)S(1)}, bf16[512,512]{1,0:T(8,128)(2,1)S(1)}, u32[]{:S(2)}, u32[]{:S(2)}) collective-permute-start(bf16[512,512]{1,0:T(8,128)(2,1)S(1)} %collective-permute-done.1.refs_3_), channel_id=1, source_target_pairs={{8,0},{12,4},{16,24},{20,28},{9,1},{13,5},{17,25},{21,29}} | collective-permute-start | bytes 1572872 | tf_op jit(solution)/shard_map/ppermute | solution.py:255
  73.2 53.7 %collective-permute-start.2 = (bf16[512,512]{1,0:T(8,128)(2,1)S(1)}, bf16[512,512]{1,0:T(8,128)(2,1)S(1)}, u32[]{:S(2)}, u32[]{:S(2)}) collective-permute-start(bf16[512,512]{1,0:T(8,128)(2,1)S(1)} %collective-permute-done.1.refs_3_), channel_id=1, source_target_pairs={{10,2},{14,6},{18,26},{22,30},{11,3},{15,7},{19,27},{23,31}} | collective-permute-start | bytes 1572872 | tf_op jit(solution)/shard_map/ppermute | solution.py:255
  74.9 47.5 %collective-permute-start.6 = (bf16[1024,128]{1,0:T(8,128)(2,1)}, bf16[1024,128]{1,0:T(8,128)(2,1)S(1)}, u32[]{:S(2)}, u32[]{:S(2)}) collective-permute-start(bf16[1024,128]{1,0:T(8,128)(2,1)} %copy-done.6), channel_id=1, source_target_pairs={{8,0},{16,24},{9,1},{17,25},{10,2},{18,26},{11,3},{19,27},{12,4},{... | collective-permute-start | bytes 786440 | tf_op jit(solution)/shard_map/ppermute | solution.py:262
  76.2 6.3 %copy-start.5 = (bf16[1024,128]{1,0:T(8,128)(2,1)S(1)}, bf16[1024,128]{1,0:T(8,128)(2,1)}, u32[]{:S(2)}) copy-start(bf16[1024,128]{1,0:T(8,128)(2,1)} %copy-done.4) | copy-start | bytes 786436
  83.4 12.9 %copy-start.7 = (bf16[1024,128]{1,0:T(8,128)(2,1)S(1)}, bf16[1024,128]{1,0:T(8,128)(2,1)}, u32[]{:S(2)}) copy-start(bf16[1024,128]{1,0:T(8,128)(2,1)} %copy-done.6) | copy-start | bytes 786436
  83.4 12.9 %copy-start.9 = (bf16[1024,128]{1,0:T(8,128)(2,1)S(1)}, bf16[1024,128]{1,0:T(8,128)(2,1)}, u32[]{:S(2)}) copy-start(bf16[1024,128]{1,0:T(8,128)(2,1)} %copy-done.8) | copy-start | bytes 786436
  (7 other events, 11.8 us)
